TPU v7x, 32 devices: a whole 2x2x4 slice. The times are simulated.
32 devices in a mesh: tm: 16 (over z, x, core), chan: 2 (over y).
Axes of the slice: x: 2, y: 2, z: 4, core: 2. Of those that a mesh axis runs over, the one named last changes fastest.
Arguments:
- random_forcing: bfloat16 [6144, 4096], P('tm', 'chan'), may hold values from -6 to 6
- eigen_root_table: float32 [768, 4096], P(None, 'chan'), may hold values from 0.1 to 2
- lane_fading_speed: float32 [4096], P('chan'), may hold values from 3.2552083e-07 to 0.025, as said below
- sudden_shrink: float32 [6144], P('tm'), may hold values from 0.125 to 1, as said below
Outputs:
- sample: float32 [6144, 4096], P('tm', 'chan')
Inputs may be any that keep to these rules, and one draw needn't show every extreme that they name: `lane_fading_speed`: every channel's rate is positive. `sudden_shrink`: every entry lies in (0, 1], and the product of all entries is at most 0.52.
All inputs are finite; a program needn't handle non-finite values.
Results may differ from a plain program's by a relative error of at most 0.0003.
Values may be sent and summed in bfloat16 or wider, within the bound.
No kernel may reach another device: no remote copies, remote signals or barrier semaphores. Data moves between devices by JAX's collectives and lax.ppermute only.
A program may use at most 192 MiB of HBM per device.

v0:
```python
import functools

import jax
import jax.numpy as jnp
import numpy as np
from jax import lax
from jax.experimental import pallas as pl
from jax.experimental.pallas import tpu as pltpu
from jax.sharding import PartitionSpec as P

LANES = 128
SEGMENTS = 8
BLOCK = 512
NYQUIST_ROWS = 16


def split(table):
    high = table.astype(jnp.bfloat16)
    low = (table - high.astype(np.float64)).astype(jnp.bfloat16)
    return high, low


def tripled(table):
    high, low = split(table)
    return np.concatenate([high, high, low], axis=1)


def tables(length):
    full = 2 * length
    half = length // 2
    frequency = 2 * np.arange(half)[:, None]
    nyquist = np.full((1, 1), length)

    def angle(frequencies, times):
        return (frequencies * times[None, :] % full) * (2.0 * np.pi / full)

    def parts(times):
        blank = np.zeros((NYQUIST_ROWS - 1, times.size))
        return (
            np.concatenate([np.cos(angle(frequency, times)), np.cos(angle(nyquist, times)), blank]),
            np.sin(angle(frequency, times)),
            np.cos(angle(frequency + 1, times)),
            np.sin(angle(frequency + 1, times)),
        )

    forward = np.concatenate(split(np.concatenate(parts(np.arange(length)))), axis=1)
    ticks = np.arange(length)
    counted = np.where(ticks < half, ticks, length - 1 - ticks)
    segment = half // SEGMENTS
    times = (np.arange(segment + 1)[:, None] + segment * np.arange(SEGMENTS)[None, :]).reshape(-1)
    even_cos, even_sin, odd_cos, odd_sin = (tripled(part.T / full) for part in parts(times))
    sums = np.concatenate([even_cos, odd_sin], axis=1)
    differences = np.concatenate([even_sin, odd_cos], axis=1)
    rows = counted // segment == np.arange(SEGMENTS)[:, None]
    blocks = counted % segment + np.where(ticks < half, 0, segment)
    blocks = blocks[:, None] == np.arange(2 * segment)
    return (
        forward, even_cos, even_sin, odd_cos, odd_sin, sums, differences,
        rows.astype(np.float32), blocks.astype(np.float32),
    )


def dot(left, right):
    return jnp.dot(left, right, preferred_element_type=jnp.float32)


def stacked(values):
    high = values.astype(jnp.bfloat16)
    low = (values - high.astype(jnp.float32)).astype(jnp.bfloat16)
    return jnp.concatenate([high, low, high], axis=0)


def spectra(section, evens, nyquist, odds, forward_ref):
    half = section.shape[0] // 2
    doubled = jnp.concatenate([section, section], axis=0)
    first = half + NYQUIST_ROWS
    scale = jnp.concatenate(
        [evens, jnp.broadcast_to(nyquist, (NYQUIST_ROWS, evens.shape[1]))], axis=0
    )
    even_cos = stacked(dot(forward_ref[:first], doubled) * scale)
    starts = (first, first + half, first + 2 * half)
    even_sin, odd_cos, odd_sin = (
        stacked(dot(forward_ref[at : at + half], doubled) * scale)
        for at, scale in zip(starts, (evens, odds, odds))
    )
    return even_cos, even_sin, odd_cos, odd_sin


def turned(x):
    row = lax.broadcasted_iota(jnp.int32, x.shape, 0)
    return jnp.take_along_axis(x, SEGMENTS - 1 - row, axis=0, mode="promise_in_bounds")


def mirrored(table_ref):
    full = table_ref.shape[0]
    half = full // 4
    row = lax.broadcasted_iota(jnp.int32, (SEGMENTS, LANES), 0)
    evens, odds = [], []
    for block in range(half // SEGMENTS):
        near = 2 * SEGMENTS * block
        direct = table_ref[pl.ds(near, SEGMENTS, stride=2), :]
        if block == 0:
            mirror = turned(table_ref[pl.ds(full - 2 * SEGMENTS, SEGMENTS, stride=2), :])
            mirror = jnp.where(row == 0, 0.0, pltpu.roll(mirror, 1, 0))
        else:
            mirror = turned(table_ref[pl.ds(full - near - 14, SEGMENTS, stride=2), :])
        evens.append(direct + mirror)
        direct = table_ref[pl.ds(near + 1, SEGMENTS, stride=2), :]
        mirror = turned(table_ref[pl.ds(full - near - 15, SEGMENTS, stride=2), :])
        odds.append(-(direct + mirror))
    return (
        jnp.concatenate(evens, axis=0),
        jnp.concatenate(odds, axis=0),
        table_ref[pl.ds(2 * half, 1), :],
    )


def wide(column, columns):
    return jnp.concatenate([column] * (columns // LANES), axis=1)


def one_minus_exp(x):
    series = jnp.ones_like(x)
    for term in range(9, 1, -1):
        series = 1.0 - x * series * (1.0 / term)
    return jnp.where(x < 0.4, x * series, 1.0 - jnp.exp(-x))


def spread(burst_ref, rows_ref, blocks_ref, out_ref):
    placed = jnp.dot(
        rows_ref[...] * burst_ref[...].reshape(1, -1), blocks_ref[...],
        precision=lax.Precision.HIGHEST, preferred_element_type=jnp.float32,
    )
    for block in range(placed.shape[1]):
        out_ref[pl.ds(block * SEGMENTS, SEGMENTS), :] = jnp.broadcast_to(
            placed[:, block : block + 1], (SEGMENTS, LANES)
        )


def orders(blocks):
    return (
        (range(blocks // 2), range(SEGMENTS)),
        (range(blocks - 1, blocks // 2 - 1, -1), range(SEGMENTS - 1, -1, -1)),
    )


def rows_of(block):
    return pl.ds(block * SEGMENTS, SEGMENTS)


def columns_of(step):
    return pl.ds(pl.multiple_of(step * BLOCK, BLOCK), BLOCK)


def scan(series, factors_ref, keep, fresh, states_ref=None):
    columns = keep.shape[1]
    entering = jnp.zeros((1, columns), jnp.float32)
    for order, rows in orders(factors_ref.shape[0] // SEGMENTS):
        state = decay = None
        for block in order:
            burst = factors_ref[rows_of(block), :]
            power = burst * burst
            variance = wide(1.0 - power, columns) + wide(power, columns) * fresh
            kick = variance * lax.rsqrt(variance) * series(block)
            factor = wide(burst, columns) * keep
            state = kick if state is None else factor * state + kick
            decay = factor if decay is None else factor * decay
            if states_ref is not None:
                states_ref[rows_of(block), :] = state
        before = [None] * SEGMENTS
        for row in rows:
            before[row] = entering
            entering = decay[row : row + 1] * entering + state[row : row + 1]
        if states_ref is not None:
            value = jnp.concatenate(before, axis=0)
            for block in order:
                value = wide(factors_ref[rows_of(block), :], columns) * keep * value
                states_ref[rows_of(block), :] += value
    return entering


def own_kernel(section_ref, *refs):
    count = BLOCK // LANES
    quarter_refs = refs[:count]
    rate_ref, burst_ref, rows_ref, blocks_ref = refs[count : count + 4]
    sources = refs[count + 4 : count + 11]
    (
        series_ref, after_ref, scale_ref, ends_ref, factors_ref, gains_ref,
        rows_kept_ref, blocks_kept_ref, *kept,
    ) = refs[count + 11 : count + 22]
    *own_tables, semaphores = refs[count + 22 :]
    even_cos_ref, even_sin_ref, odd_cos_ref, odd_sin_ref = own_tables
    forward_ref, sums_ref, differences_ref = kept
    targets = (forward_ref, *own_tables, sums_ref, differences_ref)
    copies = [
        pltpu.make_async_copy(source, target, semaphores.at[place])
        for place, (source, target) in enumerate(zip(sources, targets))
    ]
    step = pl.program_id(0)

    @pl.when(step == 0)
    def _():
        for copy in copies:
            copy.start()
        spread(burst_ref, rows_ref, blocks_ref, factors_ref)
        rows_kept_ref[...] = rows_ref[...]
        blocks_kept_ref[...] = blocks_ref[...]
        for copy in copies[:-2]:
            copy.wait()

    @pl.when(step == pl.num_programs(0) - 1)
    def _():
        for copy in copies[-2:]:
            copy.wait()

    series_ref, after_ref, scale_ref = (x.at[step] for x in (series_ref, after_ref, scale_ref))
    length, columns = section_ref.shape
    half = length // 2
    segment = half // SEGMENTS
    evens, odds, nyquist = (
        jnp.concatenate(part, axis=1) for part in zip(*map(mirrored, quarter_refs))
    )
    scale_ref[pl.ds(0, half), :] = evens
    scale_ref[pl.ds(half, half), :] = odds
    scale_ref[pl.ds(length, SEGMENTS), :] = jnp.broadcast_to(nyquist, (SEGMENTS, columns))
    even_cos, even_sin, odd_cos, odd_sin = (
        dot(table_ref[...], part)
        for table_ref, part in zip(
            own_tables, spectra(section_ref[...], evens, nyquist, odds, forward_ref)
        )
    )
    for block in range(segment + 1):
        at = slice(block * SEGMENTS, (block + 1) * SEGMENTS)
        ec, es, oc, os = even_cos[at], even_sin[at], odd_cos[at], odd_sin[at]
        if block < segment:
            even, odd = ec + es, oc + os
            series_ref[rows_of(block), :] = even - odd
            after_ref[rows_of(block), :] = even + odd
        if block > 0:
            even, odd = ec - es, os - oc
            series_ref[rows_of(segment + block - 1), :] = even - odd
            after_ref[rows_of(segment + block - 1), :] = even + odd
    rate = rate_ref[...]
    keep = jnp.exp(-rate)
    fresh = one_minus_exp(2.0 * rate)
    at = columns_of(step)
    gains_ref[pl.ds(0, 1), at] = keep
    gains_ref[pl.ds(1, 1), at] = fresh
    ends_ref[pl.ds(0, 1), at] = scan(
        lambda block: series_ref[rows_of(block), :], factors_ref, keep, fresh
    )
    logs = jnp.sum(jnp.log(factors_ref[...]), axis=0, keepdims=True)
    ends_ref[pl.ds(1, 1), at] = jnp.exp(wide(logs, columns) - length * rate)


def next_kernel(after_ref, ends_ref, gains_ref, burst_ref, rows_ref, blocks_ref, out_ref, factors_ref):
    step = pl.program_id(0)

    @pl.when(step == 0)
    def _():
        spread(burst_ref, rows_ref, blocks_ref, factors_ref)

    after_ref = after_ref.at[step]
    columns = after_ref.shape[1]
    at = columns_of(step)
    out_ref[pl.ds(0, 1), at] = ends_ref[pl.ds(0, 1), at]
    out_ref[pl.ds(1, 1), at] = scan(
        lambda block: after_ref[rows_of(block), :], factors_ref,
        gains_ref[pl.ds(0, 1), at], gains_ref[pl.ds(1, 1), at],
    )
    out_ref[pl.ds(2, 1), at] = ends_ref[pl.ds(1, 1), at]
    out_ref[pl.ds(3, 1), at] = jnp.ones((1, columns), jnp.float32)


def merge_kernel(step, sent_ref, got_ref, *refs):
    *before_ref, out_ref, after_ref = refs
    later = (lax.axis_index("tm") // step) % 2 == 1
    sent, got = sent_ref[...], got_ref[...]
    low = jnp.where(later, got, sent)
    high = jnp.where(later, sent, got)
    out_ref[pl.ds(0, 1), :] = high[:1] + high[2:3] * low[:1] + high[3:] * low[1:2]
    out_ref[pl.ds(1, 1), :] = high[1:2]
    out_ref[pl.ds(2, 1), :] = high[2:3] * low[2:3]
    out_ref[pl.ds(3, 1), :] = high[2:3] * low[3:]
    if before_ref:
        before, decay, decay_later = (before_ref[0][pl.ds(row, 1), :] for row in range(3))
    else:
        decay = jnp.ones_like(sent[:1])
        before = decay_later = jnp.zeros_like(decay)
    added = before + decay * got[:1] + decay_later * got[1:2]
    after_ref[pl.ds(0, 1), :] = jnp.where(later, added, before)
    after_ref[pl.ds(1, 1), :] = jnp.where(later, decay * got[2:3], decay)
    after_ref[pl.ds(2, 1), :] = jnp.where(later, decay * got[3:], decay_later)


def middle_kernel(
    first, section_ref, gains_ref, scale_ref, series_ref, factors_ref, forward_ref, sums_ref,
    differences_ref, *refs,
):
    *_, states_ref, work_ref = refs
    step = first + pl.program_id(0)
    at_columns = columns_of(step)
    scale_ref, series_ref, states_ref = (x.at[step] for x in (scale_ref, series_ref, states_ref))
    length = section_ref.shape[0]
    half = length // 2
    segment = half // SEGMENTS
    even_cos, even_sin, odd_cos, odd_sin = spectra(
        section_ref[:, at_columns],
        scale_ref[pl.ds(0, half), :],
        scale_ref[pl.ds(length, 1), :],
        scale_ref[pl.ds(half, half), :],
        forward_ref,
    )
    sums = dot(sums_ref[...], jnp.concatenate([even_cos, odd_sin], axis=0))
    differences = dot(differences_ref[...], jnp.concatenate([even_sin, odd_cos], axis=0))
    for block in range(segment + 1):
        at = slice(block * SEGMENTS, (block + 1) * SEGMENTS)
        if block < segment:
            place = rows_of(block)
            work_ref[place, :] = sums[at] + differences[at] + series_ref[place, :]
        if block > 0:
            place = rows_of(segment + block - 1)
            work_ref[place, :] = sums[at] - differences[at] + series_ref[place, :]
    scan(
        lambda block: work_ref[rows_of(block), :], factors_ref,
        gains_ref[pl.ds(0, 1), at_columns], gains_ref[pl.ds(1, 1), at_columns], states_ref,
    )


def last_kernel(states_ref, gains_ref, factors_ref, sent_ref, before_ref, out_ref, order_ref):
    step = pl.program_id(0)
    at = columns_of(step)
    states_ref = states_ref.at[step]
    length, columns = states_ref.shape
    blocks = length // SEGMENTS
    segment = blocks // 2
    keep = gains_ref[pl.ds(0, 1), at]
    state, spill, total, later = (sent_ref[pl.ds(row, 1), at] for row in range(4))
    before, decay, decay_later = (before_ref[pl.ds(row, 1), at] for row in range(3))
    opening = (state + later * spill) / (1.0 - total)
    entering = before + decay * opening + decay_later * spill
    for order, rows in orders(blocks):
        decay = None
        for block in order:
            factor = wide(factors_ref[rows_of(block), :], columns) * keep
            decay = factor if decay is None else factor * decay
        values = [None] * SEGMENTS
        for row in rows:
            values[row] = entering
            entering = decay[row : row + 1] * entering
        value = jnp.concatenate(values, axis=0)
        for block in order:
            value = wide(factors_ref[rows_of(block), :], columns) * keep * value
            result = states_ref[rows_of(block), :] + value
            if block < segment:
                first = block
            else:
                result = turned(result)
                first = length - 1 - (block - segment) - (SEGMENTS - 1) * segment
            for lane in range(columns // LANES):
                order_ref[lane, pl.ds(first, SEGMENTS, stride=segment), :] = result[
                    :, lane * LANES : (lane + 1) * LANES
                ]
    for lane in range(columns // LANES):
        out_ref[:, lane * LANES : (lane + 1) * LANES] = order_ref[lane]


VMEM = pl.BlockSpec(memory_space=pltpu.VMEM)
HBM = pl.BlockSpec(memory_space=pltpu.HBM)


def whole(array):
    return pl.BlockSpec(array.shape, lambda i: (0,) * array.ndim)


def blocks(rows):
    return pl.BlockSpec((rows, BLOCK), lambda i: (0, i))


def quarters(rows):
    count = BLOCK // LANES
    return [
        pl.BlockSpec((rows, LANES), lambda i, place=place: (0, count * i + place))
        for place in range(count)
    ]


def in_hbm(array):
    return pltpu.with_memory_space_constraint(array, pltpu.HBM)


def cost(flops):
    return pl.CostEstimate(flops=flops, bytes_accessed=2**24, transcendentals=0)


def params(mebibytes):
    return pltpu.CompilerParams(vmem_limit_bytes=mebibytes * 2**20)


def shards(constants, random_forcing, eigen_root_table, lane_fading_speed, sudden_shrink):
    tables, (rows, places) = constants[:7], constants[7:]
    length, channels = random_forcing.shape
    count = lax.axis_size("tm")
    steps = channels // BLOCK
    ahead = [(i, (i + 1) % count) for i in range(count)]
    back = [((i + 1) % count, i) for i in range(count)]
    rate = lane_fading_speed[None, :]
    work = 2 * channels * length * length

    previous = lax.ppermute(random_forcing, "tm", ahead)
    following = lax.ppermute(sudden_shrink, "tm", back)

    def vmem(*shape, dtype=jnp.float32):
        return pltpu.VMEM(shape, dtype)

    def kept(table):
        return vmem(*table.shape, dtype=table.dtype)

    (
        series, after, scale, ends, factors, gains, rows, places, *middle_tables
    ) = pl.pallas_call(
        own_kernel,
        grid=(steps,),
        in_specs=[
            blocks(length), *quarters(2 * length), blocks(1), whole(sudden_shrink),
            whole(rows), whole(places), *[HBM] * 7,
        ],
        out_specs=[VMEM] * 11,
        out_shape=[
            vmem(steps, length, BLOCK), vmem(steps, length, BLOCK),
            vmem(steps, length + SEGMENTS, BLOCK), vmem(SEGMENTS, channels),
            vmem(length, LANES), vmem(SEGMENTS, channels),
            *map(kept, (rows, places, tables[0], *tables[5:])),
        ],
        scratch_shapes=[
            *(kept(table) for table in tables[1:5]), pltpu.SemaphoreType.DMA((7,)),
        ],
        compiler_params=params(36),
        cost_estimate=cost(7 * work),
        name="own",
    )(
        *map(
            in_hbm,
            (
                random_forcing, *[eigen_root_table] * (BLOCK // LANES), rate, sudden_shrink,
                rows, places, *tables,
            ),
        )
    )

    sent = pl.pallas_call(
        next_kernel,
        grid=(steps,),
        in_specs=[VMEM] * 6,
        out_specs=VMEM,
        out_shape=vmem(4, channels),
        scratch_shapes=[vmem(length, LANES)],
        compiler_params=params(16),
        cost_estimate=cost(work),
        name="next",
    )(after, ends, gains, following, rows, places)

    states = ()
    for part in range(2):
        states = (
            pl.pallas_call(
                functools.partial(middle_kernel, part * steps // 2),
                grid=(steps // 2,),
                in_specs=[VMEM] * (8 + len(states)),
                out_specs=VMEM,
                out_shape=vmem(steps, length, BLOCK),
                scratch_shapes=[vmem(length, BLOCK)],
                input_output_aliases={8: 0} if states else {},
                compiler_params=params(24),
                cost_estimate=cost(4 * work),
                name="middle",
            )(previous, gains, scale, series, factors, *middle_tables, *states),
        )
    (states,) = states

    before = None
    step = 1
    while step < count:
        got = lax.ppermute(sent, "tm", [(i, i ^ step) for i in range(count)])
        kept_rows = () if before is None else (before,)
        sent, before = pl.pallas_call(
            functools.partial(merge_kernel, step),
            in_specs=[VMEM] * (2 + len(kept_rows)),
            out_specs=[VMEM] * 2,
            out_shape=[vmem(4, channels), vmem(3, channels)],
            compiler_params=params(4),
            cost_estimate=cost(channels),
            name="merge",
        )(sent, got, *kept_rows)
        step *= 2

    return pl.pallas_call(
        last_kernel,
        grid=(steps,),
        in_specs=[VMEM] * 5,
        out_specs=blocks(length),
        out_shape=pltpu.HBM((length, channels), jnp.float32),
        scratch_shapes=[vmem(BLOCK // LANES, length, LANES)],
        compiler_params=params(16),
        cost_estimate=cost(work),
        name="last",
    )(states, gains, factors, sent, before)


def solution(mesh):
    placed = (P("tm", "chan"), P(None, "chan"), P("chan"), P("tm"))

    def program(random_forcing, eigen_root_table, lane_fading_speed, sudden_shrink):
        length = random_forcing.shape[0] // mesh.shape["tm"]
        constants = tuple(jnp.asarray(table) for table in tables(length))

        def body(*args):
            return shards(args[:-4], *args[-4:])

        return jax.shard_map(
            body, mesh=mesh, in_specs=(P(None, None),) * len(constants) + placed,
            out_specs=P("tm", "chan"), check_vma=False,
        )(*constants, random_forcing, eigen_root_table, lane_fading_speed, sudden_shrink)

    return program
```

profile of v0, /device:TPU:0, one launch (start us, length us, event | category | flops | bytes accessed | tf_op | source)
XLA Modules:
  0.0 43.5 jit_solution(3602750593348819847)
XLA Ops:
  0.0 0.5 %collective-permute-start = (bf16[384,2048]{1,0:T(8,128)(2,1)}, bf16[384,2048]{1,0:T(8,128)(2,1)S(1)}, u32[]{:S(2)}, u32[]{:S(2)}) collective-permute-start(bf16[384,2048]{1,0:T(8,128)(2,1)} %section_ref.1), channel_id=1, source_target_pairs={{0,2},{2,4},{4,6},{6,8},{8,10},{10,12},{12,14},{14,16},{16,18},{18... | collective-permute-start | bytes 4718600 | tf_op jit(solution)/shard_map/ppermute | solution.py:410
  0.5 5.0 %collective-permute-start.1 = (f32[384]{0:T(512)}, f32[384]{0:T(512)S(1)}, u32[]{:S(2)}, u32[]{:S(2)}) collective-permute-start(f32[384]{0:T(512)} %refs_5_.1), channel_id=1, source_target_pairs={{2,0},{4,2},{6,4},{8,6},{10,8},{12,10},{14,12},{16,14},{18,16},{20... | collective-permute-start | bytes 4616 | tf_op jit(solution)/shard_map/ppermute | solution.py:411
  5.4 11.1 %own.1 = (f32[4,384,512]{2,1,0:T(8,128)S(1)}, f32[4,384,512]{2,1,0:T(8,128)S(1)}, f32[4,392,512]{2,1,0:T(8,128)S(1)}, f32[8,2048]{1,0:T(8,128)S(1)}, f32[384,128...) custom-call(bf16[384,2048]{1,0:T(8,128)(2,1)} %section_ref.1, ...), custom_call_target="tpu_custom_call" | custom-call | flops 4227858432 | bytes 16777216 | tf_op jit(solution)/shard_map/own/pallas_call | solution.py:421
  16.5 0.0 collective-permute-done.1.burst_ref
  16.5 1.6 %next.1.sent_ref = f32[4,2048]{1,0:T(4,128)S(1)} custom-call(f32[4,384,512]{2,1,0:T(8,128)S(1)} %get-tuple-element.31.after_ref, f32[8,2048]{1,0:T(8,128)S(1)} %get-tuple-element.32.ends_ref, f32[8,2048]{1,0:T(8,128)S(1)} %get-tuple-element.24.gains_ref, f32[384]{0:T(512)S(1)} %collective-permute-done.1.burst_ref, f32[8,384]{1,0:T(8,128)S(1)} %get-tuple-element.33.rows_ref, ...), custom_call_target="tpu_custom_call" | custom-call | flops 603979776 | bytes 16777216 | tf_op jit(solution)/shard_map/next/pallas_call | solution.py:451
  18.1 0.1 collective-permute-start.2
  18.2 1.2 %collective-permute-done.2.got_ref = f32[4,2048]{1,0:T(4,128)S(1)} collective-permute-done((f32[4,2048]{1,0:T(4,128)S(1)}, f32[4,2048]{1,0:T(4,128)S(1)}, u32[]{:S(2)}, u32[]{:S(2)}) %collective-permute-start.2) | collective-permute-done | bytes 32800 | tf_op jit(solution)/shard_map/ppermute | solution.py:484
  19.4 0.1 collective-permute-start.3
  19.5 4.9 %collective-permute-done.3.got_ref = f32[4,2048]{1,0:T(4,128)S(1)} collective-permute-done((f32[4,2048]{1,0:T(4,128)S(1)}, f32[4,2048]{1,0:T(4,128)S(1)}, u32[]{:S(2)}, u32[]{:S(2)}) %collective-permute-start.3) | collective-permute-done | bytes 32800 | tf_op jit(solution)/shard_map/ppermute | solution.py:484
  24.5 0.3 collective-permute-start.4
  24.8 3.6 %collective-permute-done.4.got_ref = f32[4,2048]{1,0:T(4,128)S(1)} collective-permute-done((f32[4,2048]{1,0:T(4,128)S(1)}, f32[4,2048]{1,0:T(4,128)S(1)}, u32[]{:S(2)}, u32[]{:S(2)}) %collective-permute-start.4) | collective-permute-done | bytes 32800 | tf_op jit(solution)/shard_map/ppermute | solution.py:484
  28.5 1.4 %collective-permute-start.5 = (f32[4,2048]{1,0:T(4,128)S(1)}, f32[4,2048]{1,0:T(4,128)S(1)}, u32[]{:S(2)}, u32[]{:S(2)}) collective-permute-start(f32[4,2048]{1,0:T(4,128)S(1)} %get-tuple-element.39.sent_ref), channel_id=1, source_target_pairs={{0,16},{2,18},{4,20},{6,22},{8,24},{10,26},{12,28},{14,30},{16,0},... | collective-permute-start | bytes 98312 | tf_op jit(solution)/shard_map/ppermute | solution.py:484
  29.9 3.6 %collective-permute-done.5.got_ref = f32[4,2048]{1,0:T(4,128)S(1)} collective-permute-done((f32[4,2048]{1,0:T(4,128)S(1)}, f32[4,2048]{1,0:T(4,128)S(1)}, u32[]{:S(2)}, u32[]{:S(2)}) %collective-permute-start.5) | collective-permute-done | bytes 32800 | tf_op jit(solution)/shard_map/ppermute | solution.py:484
  33.5 0.0 collective-permute-done.section_ref
  33.5 3.6 %middle.2.refs_0_ = f32[4,384,512]{2,1,0:T(8,128)S(1)} custom-call(bf16[384,2048]{1,0:T(8,128)(2,1)S(1)} %collective-permute-done.section_ref, f32[8,2048]{1,0:T(8,128)S(1)} %get-tuple-element.24.gains_ref, f32[4,392,512]{2,1,0:T(8,128)S(1)} %get-tuple-element.25.scale_ref, f32[4,384,512]{2,1,0:T(8,128)S(1)} %get-tuple-element.26.series_ref, ...), custom_call_target="tpu_custom_call" | custom-call | flops 2415919104 | bytes 16777216 | tf_op jit(solution)/shard_map/middle/pallas_call | solution.py:466
  37.2 3.6 %middle.3.states_ref = f32[4,384,512]{2,1,0:T(8,128)S(1)} custom-call(bf16[384,2048]{1,0:T(8,128)(2,1)S(1)} %collective-permute-done.section_ref, f32[8,2048]{1,0:T(8,128)S(1)} %get-tuple-element.24.gains_ref, f32[4,392,512]{2,1,0:T(8,128)S(1)} %get-tuple-element.25.scale_ref, ...), custom_call_target="tpu_custom_call", output_to_operand_aliasing={{}: (8, {})} | custom-call | flops 2415919104 | bytes 16777216 | tf_op jit(solution)/shard_map/middle/pallas_call | solution.py:466
  40.8 2.8 %last.1 = f32[384,2048]{1,0:T(8,128)} custom-call(f32[4,384,512]{2,1,0:T(8,128)S(1)} %middle.3.states_ref, f32[8,2048]{1,0:T(8,128)S(1)} %get-tuple-element.24.gains_ref, f32[384,128]{1,0:T(8,128)S(1)} %get-tuple-element.27.factors_ref, f32[4,2048]{1,0:T(4,128)S(1)} %get-tuple-element.41.sent_ref, f32[3,2048]{1,0:T(4,128)S(1)} %get-tuple-element.42.before_ref), custom_call_target="tpu_custom_call" | custom-call | flops 603979776 | bytes 16777216 | tf_op jit(solution)/shard_map/last/pallas_call | solution.py:497
  (4 shorter events, 0.2 us)
Async XLA Ops:
  0.0 33.5 %collective-permute-start = (bf16[384,2048]{1,0:T(8,128)(2,1)}, bf16[384,2048]{1,0:T(8,128)(2,1)S(1)}, u32[]{:S(2)}, u32[]{:S(2)}) collective-permute-start(bf16[384,2048]{1,0:T(8,128)(2,1)} %section_ref.1), channel_id=1, source_target_pairs={{0,2},{2,4},{4,6},{6,8},{8,10},{10,12},{12,14},{14,16},{16,18},{18... | collective-permute-start | bytes 4718600 | tf_op jit(solution)/shard_map/ppermute | solution.py:410
  0.5 16.0 %collective-permute-start.1 = (f32[384]{0:T(512)}, f32[384]{0:T(512)S(1)}, u32[]{:S(2)}, u32[]{:S(2)}) collective-permute-start(f32[384]{0:T(512)} %refs_5_.1), channel_id=1, source_target_pairs={{2,0},{4,2},{6,4},{8,6},{10,8},{12,10},{14,12},{16,14},{18,16},{20... | collective-permute-start | bytes 4616 | tf_op jit(solution)/shard_map/ppermute | solution.py:411
  18.1 1.3 %collective-permute-start.2 = (f32[4,2048]{1,0:T(4,128)S(1)}, f32[4,2048]{1,0:T(4,128)S(1)}, u32[]{:S(2)}, u32[]{:S(2)}) collective-permute-start(f32[4,2048]{1,0:T(4,128)S(1)} %next.1.sent_ref), channel_id=1, source_target_pairs={{0,2},{2,0},{4,6},{6,4},{8,10},{10,8},{12,14},{14,12},{16,18},{18,... | collective-permute-start | bytes 98312 | tf_op jit(solution)/shard_map/ppermute | solution.py:484
  19.4 5.0 %collective-permute-start.3 = (f32[4,2048]{1,0:T(4,128)S(1)}, f32[4,2048]{1,0:T(4,128)S(1)}, u32[]{:S(2)}, u32[]{:S(2)}) collective-permute-start(f32[4,2048]{1,0:T(4,128)S(1)} %get-tuple-element.35.sent_ref), channel_id=1, source_target_pairs={{0,4},{2,6},{4,0},{6,2},{8,12},{10,14},{12,8},{14,10},{16,20},{18,... | collective-permute-start | bytes 98312 | tf_op jit(solution)/shard_map/ppermute | solution.py:484
  24.5 4.0 %collective-permute-start.4 = (f32[4,2048]{1,0:T(4,128)S(1)}, f32[4,2048]{1,0:T(4,128)S(1)}, u32[]{:S(2)}, u32[]{:S(2)}) collective-permute-start(f32[4,2048]{1,0:T(4,128)S(1)} %get-tuple-element.37.sent_ref), channel_id=1, source_target_pairs={{0,8},{2,10},{4,12},{6,14},{8,0},{10,2},{12,4},{14,6},{16,24},{18,... | collective-permute-start | bytes 98312 | tf_op jit(solution)/shard_map/ppermute | solution.py:484
  28.5 4.9 %collective-permute-start.5 = (f32[4,2048]{1,0:T(4,128)S(1)}, f32[4,2048]{1,0:T(4,128)S(1)}, u32[]{:S(2)}, u32[]{:S(2)}) collective-permute-start(f32[4,2048]{1,0:T(4,128)S(1)} %get-tuple-element.39.sent_ref), channel_id=1, source_target_pairs={{0,16},{2,18},{4,20},{6,22},{8,24},{10,26},{12,28},{14,30},{16,0},... | collective-permute-start | bytes 98312 | tf_op jit(solution)/shard_map/ppermute | solution.py:484
where the time goes:
time: 43.7 us; the launch traced here: 43.5 us
  Pallas kernels  22.8 us (52%)
  waiting for transfers between devices  13.4 us (31%)
  starting transfers between devices  7.28 us (17%)
    ppermute x4, waiting for transfers between devices, shards(): got = lax.ppermute(sent, 'tm', [(i, i ^ step) for i in range(count)])  13.4 us
    pallas_call x1, Pallas kernels, shards(): pl.pallas_call(own_kernel, grid=(steps,), in_specs=[blocks(length), *quar...  11.1 us
    pallas_call x2, Pallas kernels, shards(): pl.pallas_call(functools.partial(middle_kernel, part * steps // 2), grid=...  7.23 us
    ppermute x1, starting transfers between devices, shards(): following = lax.ppermute(sudden_shrink, 'tm', back)  4.95 us
    pallas_call x1, Pallas kernels, shards(): pl.pallas_call(last_kernel, grid=(steps,), in_specs=[VMEM] * 5, out_specs...  2.76 us
    ppermute x4, starting transfers between devices, shards(): got = lax.ppermute(sent, 'tm', [(i, i ^ step) for i in range(count)])  1.83 us
    pallas_call x1, Pallas kernels, shards(): pl.pallas_call(next_kernel, grid=(steps,), in_specs=[VMEM] * 6, out_specs...  1.57 us
  transfers between devices with their start and end apart: 6, of which 4 were waited for; matrix products, arithmetic and copies ran while one was open for 0% of the time, Pallas kernels for 29%

commit v1 on v0

--- a/solution.py
+++ b/solution.py
@@ -49,13 +49,11 @@
     segment = half // SEGMENTS
     times = (np.arange(segment + 1)[:, None] + segment * np.arange(SEGMENTS)[None, :]).reshape(-1)
     even_cos, even_sin, odd_cos, odd_sin = (tripled(part.T / full) for part in parts(times))
-    sums = np.concatenate([even_cos, odd_sin], axis=1)
-    differences = np.concatenate([even_sin, odd_cos], axis=1)
     rows = counted // segment == np.arange(SEGMENTS)[:, None]
     blocks = counted % segment + np.where(ticks < half, 0, segment)
     blocks = blocks[:, None] == np.arange(2 * segment)
     return (
-        forward, even_cos, even_sin, odd_cos, odd_sin, sums, differences,
+        forward, even_cos, even_sin, odd_cos, odd_sin,
         rows.astype(np.float32), blocks.astype(np.float32),
     )
 
@@ -152,7 +150,7 @@
     return pl.ds(pl.multiple_of(step * BLOCK, BLOCK), BLOCK)
 
 
-def scan(series, factors_ref, keep, fresh, states_ref=None):
+def scan(series, factors_ref, keep, fresh, states_ref=None, store=None):
     columns = keep.shape[1]
     entering = jnp.zeros((1, columns), jnp.float32)
     for order, rows in orders(factors_ref.shape[0] // SEGMENTS):
@@ -175,82 +173,134 @@
             value = jnp.concatenate(before, axis=0)
             for block in order:
                 value = wide(factors_ref[rows_of(block), :], columns) * keep * value
-                states_ref[rows_of(block), :] += value
+                store(block, states_ref[rows_of(block), :] + value)
     return entering
 
 
-def own_kernel(section_ref, *refs):
-    count = BLOCK // LANES
-    quarter_refs = refs[:count]
-    rate_ref, burst_ref, rows_ref, blocks_ref = refs[count : count + 4]
-    sources = refs[count + 4 : count + 11]
-    (
-        series_ref, after_ref, scale_ref, ends_ref, factors_ref, gains_ref,
-        rows_kept_ref, blocks_kept_ref, *kept,
-    ) = refs[count + 11 : count + 22]
-    *own_tables, semaphores = refs[count + 22 :]
-    even_cos_ref, even_sin_ref, odd_cos_ref, odd_sin_ref = own_tables
-    forward_ref, sums_ref, differences_ref = kept
-    targets = (forward_ref, *own_tables, sums_ref, differences_ref)
+def load_kernel(section_hbm, table_hbm, rate_hbm, burst_hbm, *refs):
+    sources, refs = refs[:7], refs[7:]
+    part_refs, refs = refs[:3], refs[3:]
+    table_ref, factors_ref, powers_ref, gains_ref = refs[:4]
+    targets, (rate_ref, burst_ref, semaphores) = refs[4:11], refs[11:]
+    length, channels = section_hbm.shape
+    starts = (0, part_refs[0].shape[1], channels - part_refs[2].shape[1])
     copies = [
         pltpu.make_async_copy(source, target, semaphores.at[place])
-        for place, (source, target) in enumerate(zip(sources, targets))
+        for place, (source, target) in enumerate(
+            [(burst_hbm, burst_ref), *zip(sources[:2], targets[:2]), (rate_hbm, rate_ref)]
+            + [
+                (section_hbm.at[:, pl.ds(start, part_ref.shape[1])], part_ref)
+                for start, part_ref in zip(starts, part_refs)
+            ]
+            + [
+                (table_hbm.at[:, pl.ds(group * LANES, LANES)], table_ref.at[group])
+                for group in range(BLOCK // LANES)
+            ]
+            + list(zip(sources[2:], targets[2:]))
+        )
     ]
+    for copy in copies:
+        copy.start()
+    for copy in copies[:4]:
+        copy.wait()
+    rows_ref, blocks_ref = targets[:2]
+    spread(burst_ref, rows_ref, blocks_ref, factors_ref)
+    shape = (length, length)
+    earlier = lax.broadcasted_iota(jnp.int32, shape, 1) <= lax.broadcasted_iota(jnp.int32, shape, 0)
+    logs = jnp.where(earlier, jnp.log(burst_ref[...].reshape(1, -1)), 0.0)
+    powers_ref[...] = jnp.broadcast_to(
+        jnp.exp(jnp.sum(logs, axis=1, keepdims=True)), (length, LANES)
+    )
+    rate = rate_ref[...]
+    keep = jnp.exp(-rate)
+    gains_ref[pl.ds(0, 1), :] = keep
+    gains_ref[pl.ds(1, 1), :] = one_minus_exp(2.0 * rate)
+    total = jnp.sum(jnp.log(factors_ref[...]), axis=0, keepdims=True)
+    gains_ref[pl.ds(2, 1), :] = jnp.exp(wide(total, rate.shape[1]) - length * rate)
+    for copy in copies[4:]:
+        copy.wait()
+
+
+def own_kernel(section_hbm, table_hbm, part_ref, first_ref, factors_ref, gains_ref, forward_ref, *refs):
+    own_tables, refs = refs[:4], refs[4:]
+    series_ref, after_ref, scale_ref, ends_ref, sums_ref, differences_ref = refs[:6]
+    section_ref, table_ref, section_semaphores, table_semaphores = refs[6:]
+    even_cos_ref, even_sin_ref, odd_cos_ref, odd_sin_ref = own_tables
     step = pl.program_id(0)
+    length, channels = section_ref.shape
+    half = length // 2
+    segment = half // SEGMENTS
+    groups = BLOCK // LANES
+
+    def load_section(block):
+        return pltpu.make_async_copy(
+            section_hbm.at[:, columns_of(block)], section_ref.at[:, columns_of(block)],
+            section_semaphores.at[block],
+        )
+
+    def load_table(group):
+        columns = pl.ds(pl.multiple_of(group * LANES, LANES), LANES)
+        return pltpu.make_async_copy(
+            table_hbm.at[:, columns], table_ref.at[group], table_semaphores.at[group]
+        )
 
     @pl.when(step == 0)
     def _():
-        for copy in copies:
-            copy.start()
-        spread(burst_ref, rows_ref, blocks_ref, factors_ref)
-        rows_kept_ref[...] = rows_ref[...]
-        blocks_kept_ref[...] = blocks_ref[...]
-        for copy in copies[:-2]:
-            copy.wait()
+        for block in range(1, channels // BLOCK):
+            load_section(block).start()
+            for group in range(groups):
+                load_table(block * groups + group).start()
+        section_ref[:, :BLOCK] = part_ref[:, :BLOCK]
+        for group in range(groups):
+            table_ref[group] = first_ref[group]
 
     @pl.when(step == pl.num_programs(0) - 1)
     def _():
-        for copy in copies[-2:]:
-            copy.wait()
-
-    series_ref, after_ref, scale_ref = (x.at[step] for x in (series_ref, after_ref, scale_ref))
-    length, columns = section_ref.shape
-    half = length // 2
-    segment = half // SEGMENTS
-    evens, odds, nyquist = (
-        jnp.concatenate(part, axis=1) for part in zip(*map(mirrored, quarter_refs))
-    )
-    scale_ref[pl.ds(0, half), :] = evens
-    scale_ref[pl.ds(half, half), :] = odds
-    scale_ref[pl.ds(length, SEGMENTS), :] = jnp.broadcast_to(nyquist, (SEGMENTS, columns))
-    even_cos, even_sin, odd_cos, odd_sin = (
-        dot(table_ref[...], part)
-        for table_ref, part in zip(
-            own_tables, spectra(section_ref[...], evens, nyquist, odds, forward_ref)
-        )
-    )
-    for block in range(segment + 1):
-        at = slice(block * SEGMENTS, (block + 1) * SEGMENTS)
-        ec, es, oc, os = even_cos[at], even_sin[at], odd_cos[at], odd_sin[at]
-        if block < segment:
-            even, odd = ec + es, oc + os
-            series_ref[rows_of(block), :] = even - odd
-            after_ref[rows_of(block), :] = even + odd
-        if block > 0:
-            even, odd = ec - es, os - oc
-            series_ref[rows_of(segment + block - 1), :] = even - odd
-            after_ref[rows_of(segment + block - 1), :] = even + odd
-    rate = rate_ref[...]
-    keep = jnp.exp(-rate)
-    fresh = one_minus_exp(2.0 * rate)
-    at = columns_of(step)
-    gains_ref[pl.ds(0, 1), at] = keep
-    gains_ref[pl.ds(1, 1), at] = fresh
-    ends_ref[pl.ds(0, 1), at] = scan(
-        lambda block: series_ref[rows_of(block), :], factors_ref, keep, fresh
-    )
-    logs = jnp.sum(jnp.log(factors_ref[...]), axis=0, keepdims=True)
-    ends_ref[pl.ds(1, 1), at] = jnp.exp(wide(logs, columns) - length * rate)
+        for target, first, second in (
+            (sums_ref, even_cos_ref, odd_sin_ref), (differences_ref, even_sin_ref, odd_cos_ref)
+        ):
+            target[:, : first.shape[1]] = first[...]
+            target[:, first.shape[1] :] = second[...]
+
+    @pl.when(step > 0)
+    def _():
+        load_section(step).wait()
+        for group in range(groups):
+            load_table(step * groups + group).wait()
+
+    for block in (step,):
+        series, after, scale = (x.at[block] for x in (series_ref, after_ref, scale_ref))
+        at = columns_of(block)
+        evens, odds, nyquist = (
+            jnp.concatenate(part, axis=1)
+            for part in zip(
+                *(mirrored(table_ref.at[block * groups + group]) for group in range(groups))
+            )
+        )
+        scale[pl.ds(0, half), :] = evens
+        scale[pl.ds(half, half), :] = odds
+        scale[pl.ds(length, SEGMENTS), :] = jnp.broadcast_to(nyquist, (SEGMENTS, BLOCK))
+        even_cos, even_sin, odd_cos, odd_sin = (
+            dot(inverse_ref[...], part)
+            for inverse_ref, part in zip(
+                own_tables, spectra(section_ref[:, at], evens, nyquist, odds, forward_ref)
+            )
+        )
+        for row in range(segment + 1):
+            rows = slice(row * SEGMENTS, (row + 1) * SEGMENTS)
+            ec, es, oc, os = even_cos[rows], even_sin[rows], odd_cos[rows], odd_sin[rows]
+            if row < segment:
+                even, odd = ec + es, oc + os
+                series[rows_of(row), :] = even - odd
+                after[rows_of(row), :] = even + odd
+            if row > 0:
+                even, odd = ec - es, os - oc
+                series[rows_of(segment + row - 1), :] = even - odd
+                after[rows_of(segment + row - 1), :] = even + odd
+        ends_ref[pl.ds(0, 1), at] = scan(
+            lambda row: series[rows_of(row), :], factors_ref,
+            gains_ref[pl.ds(0, 1), at], gains_ref[pl.ds(1, 1), at],
+        )
 
 
 def next_kernel(after_ref, ends_ref, gains_ref, burst_ref, rows_ref, blocks_ref, out_ref, factors_ref):
@@ -268,7 +318,7 @@
         lambda block: after_ref[rows_of(block), :], factors_ref,
         gains_ref[pl.ds(0, 1), at], gains_ref[pl.ds(1, 1), at],
     )
-    out_ref[pl.ds(2, 1), at] = ends_ref[pl.ds(1, 1), at]
+    out_ref[pl.ds(2, 1), at] = gains_ref[pl.ds(2, 1), at]
     out_ref[pl.ds(3, 1), at] = jnp.ones((1, columns), jnp.float32)
 
 
@@ -300,12 +350,12 @@
     *_, states_ref, work_ref = refs
     step = first + pl.program_id(0)
     at_columns = columns_of(step)
-    scale_ref, series_ref, states_ref = (x.at[step] for x in (scale_ref, series_ref, states_ref))
+    scale_ref, series_ref = scale_ref.at[step], series_ref.at[step]
     length = section_ref.shape[0]
     half = length // 2
     segment = half // SEGMENTS
     even_cos, even_sin, odd_cos, odd_sin = spectra(
-        section_ref[:, at_columns],
+        section_ref[:, columns_of(step - first)],
         scale_ref[pl.ds(0, half), :],
         scale_ref[pl.ds(length, 1), :],
         scale_ref[pl.ds(half, half), :],
@@ -321,70 +371,56 @@
         if block > 0:
             place = rows_of(segment + block - 1)
             work_ref[place, :] = sums[at] - differences[at] + series_ref[place, :]
+    groups = BLOCK // LANES
+
+    def store(block, value):
+        if block < segment:
+            start = block
+        else:
+            value = turned(value)
+            start = length - 1 - (block - segment) - (SEGMENTS - 1) * segment
+        for group in range(groups):
+            states_ref[step * groups + group, pl.ds(start, SEGMENTS, stride=segment), :] = value[
+                :, group * LANES : (group + 1) * LANES
+            ]
+
     scan(
         lambda block: work_ref[rows_of(block), :], factors_ref,
-        gains_ref[pl.ds(0, 1), at_columns], gains_ref[pl.ds(1, 1), at_columns], states_ref,
-    )
-
-
-def last_kernel(states_ref, gains_ref, factors_ref, sent_ref, before_ref, out_ref, order_ref):
+        gains_ref[pl.ds(0, 1), at_columns], gains_ref[pl.ds(1, 1), at_columns], work_ref, store,
+    )
+
+
+def last_kernel(states_ref, gains_ref, powers_ref, sent_ref, before_ref, out_ref):
     step = pl.program_id(0)
     at = columns_of(step)
-    states_ref = states_ref.at[step]
-    length, columns = states_ref.shape
-    blocks = length // SEGMENTS
-    segment = blocks // 2
+    length, columns = out_ref.shape
     keep = gains_ref[pl.ds(0, 1), at]
     state, spill, total, later = (sent_ref[pl.ds(row, 1), at] for row in range(4))
     before, decay, decay_later = (before_ref[pl.ds(row, 1), at] for row in range(3))
     opening = (state + later * spill) / (1.0 - total)
     entering = before + decay * opening + decay_later * spill
-    for order, rows in orders(blocks):
-        decay = None
-        for block in order:
-            factor = wide(factors_ref[rows_of(block), :], columns) * keep
-            decay = factor if decay is None else factor * decay
-        values = [None] * SEGMENTS
-        for row in rows:
-            values[row] = entering
-            entering = decay[row : row + 1] * entering
-        value = jnp.concatenate(values, axis=0)
-        for block in order:
-            value = wide(factors_ref[rows_of(block), :], columns) * keep * value
-            result = states_ref[rows_of(block), :] + value
-            if block < segment:
-                first = block
-            else:
-                result = turned(result)
-                first = length - 1 - (block - segment) - (SEGMENTS - 1) * segment
-            for lane in range(columns // LANES):
-                order_ref[lane, pl.ds(first, SEGMENTS, stride=segment), :] = result[
-                    :, lane * LANES : (lane + 1) * LANES
-                ]
-    for lane in range(columns // LANES):
-        out_ref[:, lane * LANES : (lane + 1) * LANES] = order_ref[lane]
+    rows = []
+    for _ in range(SEGMENTS):
+        entering = keep * entering
+        rows.append(entering)
+    value = jnp.concatenate(rows, axis=0)
+    jump = keep
+    for _ in range(SEGMENTS.bit_length() - 1):
+        jump = jump * jump
+    groups = columns // LANES
+    for block in range(length // SEGMENTS):
+        place = rows_of(block)
+        states = jnp.concatenate(
+            [states_ref[step * groups + group, place, :] for group in range(groups)], axis=1
+        )
+        out_ref[place, :] = states + wide(powers_ref[place, :], columns) * value
+        value = jump * value
 
 
 VMEM = pl.BlockSpec(memory_space=pltpu.VMEM)
 HBM = pl.BlockSpec(memory_space=pltpu.HBM)
 
 
-def whole(array):
-    return pl.BlockSpec(array.shape, lambda i: (0,) * array.ndim)
-
-
-def blocks(rows):
-    return pl.BlockSpec((rows, BLOCK), lambda i: (0, i))
-
-
-def quarters(rows):
-    count = BLOCK // LANES
-    return [
-        pl.BlockSpec((rows, LANES), lambda i, place=place: (0, count * i + place))
-        for place in range(count)
-    ]
-
-
 def in_hbm(array):
     return pltpu.with_memory_space_constraint(array, pltpu.HBM)
 
@@ -398,7 +434,7 @@
 
 
 def shards(constants, random_forcing, eigen_root_table, lane_fading_speed, sudden_shrink):
-    tables, (rows, places) = constants[:7], constants[7:]
+    tables, (rows, places) = constants[:5], constants[5:]
     length, channels = random_forcing.shape
     count = lax.axis_size("tm")
     steps = channels // BLOCK
@@ -407,45 +443,63 @@
     rate = lane_fading_speed[None, :]
     work = 2 * channels * length * length
 
-    previous = lax.ppermute(random_forcing, "tm", ahead)
-    following = lax.ppermute(sudden_shrink, "tm", back)
-
     def vmem(*shape, dtype=jnp.float32):
         return pltpu.VMEM(shape, dtype)
 
     def kept(table):
         return vmem(*table.shape, dtype=table.dtype)
 
-    (
-        series, after, scale, ends, factors, gains, rows, places, *middle_tables
-    ) = pl.pallas_call(
+    def joined(pair):
+        return vmem(
+            pair[0].shape[0], sum(table.shape[1] for table in pair), dtype=pair[0].dtype
+        )
+
+    cuts = (0, steps // 2, steps - max(1, steps // 4), steps)
+    loaded = pl.pallas_call(
+        load_kernel,
+        in_specs=[HBM] * 11,
+        out_specs=[VMEM] * 14,
+        out_shape=[
+            *(
+                vmem(length, width * BLOCK, dtype=random_forcing.dtype)
+                for width in (end - start for start, end in zip(cuts, cuts[1:]))
+            ),
+            vmem(BLOCK // LANES, 2 * length, LANES), vmem(length, LANES), vmem(length, LANES),
+            vmem(SEGMENTS, channels), *map(kept, (rows, places, *tables)),
+        ],
+        scratch_shapes=[vmem(1, channels), vmem(length), pltpu.SemaphoreType.DMA((16,))],
+        compiler_params=params(8),
+        cost_estimate=cost(work // 4),
+        name="load",
+    )(*map(in_hbm, (random_forcing, eigen_root_table, rate, sudden_shrink, rows, places, *tables)))
+
+    parts, inverses = loaded[:3], loaded[10:]
+    first, factors, powers, gains, rows, places, forward = loaded[3:10]
+    previous = []
+    for part in range(3):
+        previous.append(lax.ppermute(parts[part], "tm", ahead))
+    following = lax.ppermute(sudden_shrink, "tm", back)
+
+    series, after, scale, ends, *middle_tables = pl.pallas_call(
         own_kernel,
         grid=(steps,),
-        in_specs=[
-            blocks(length), *quarters(2 * length), blocks(1), whole(sudden_shrink),
-            whole(rows), whole(places), *[HBM] * 7,
-        ],
-        out_specs=[VMEM] * 11,
+        in_specs=[HBM] * 2 + [VMEM] * 9,
+        out_specs=[VMEM] * 6,
         out_shape=[
             vmem(steps, length, BLOCK), vmem(steps, length, BLOCK),
-            vmem(steps, length + SEGMENTS, BLOCK), vmem(SEGMENTS, channels),
-            vmem(length, LANES), vmem(SEGMENTS, channels),
-            *map(kept, (rows, places, tables[0], *tables[5:])),
+            vmem(steps, length + SEGMENTS, BLOCK), vmem(1, channels),
+            *map(joined, (inverses[::3], inverses[1:3])),
         ],
         scratch_shapes=[
-            *(kept(table) for table in tables[1:5]), pltpu.SemaphoreType.DMA((7,)),
+            kept(random_forcing), vmem(channels // LANES, 2 * length, LANES),
+            pltpu.SemaphoreType.DMA((steps,)), pltpu.SemaphoreType.DMA((channels // LANES,)),
         ],
-        compiler_params=params(36),
+        compiler_params=params(22),
         cost_estimate=cost(7 * work),
         name="own",
     )(
-        *map(
-            in_hbm,
-            (
-                random_forcing, *[eigen_root_table] * (BLOCK // LANES), rate, sudden_shrink,
-                rows, places, *tables,
-            ),
-        )
+        in_hbm(random_forcing), in_hbm(eigen_root_table), parts[0], first, factors, gains,
+        forward, *inverses,
     )
 
     sent = pl.pallas_call(
@@ -461,20 +515,20 @@
     )(after, ends, gains, following, rows, places)
 
     states = ()
-    for part in range(2):
+    for part, (first, end) in enumerate(zip(cuts, cuts[1:])):
         states = (
             pl.pallas_call(
-                functools.partial(middle_kernel, part * steps // 2),
-                grid=(steps // 2,),
+                functools.partial(middle_kernel, first),
+                grid=(end - first,),
                 in_specs=[VMEM] * (8 + len(states)),
                 out_specs=VMEM,
-                out_shape=vmem(steps, length, BLOCK),
+                out_shape=vmem(channels // LANES, length, LANES),
                 scratch_shapes=[vmem(length, BLOCK)],
                 input_output_aliases={8: 0} if states else {},
                 compiler_params=params(24),
                 cost_estimate=cost(4 * work),
                 name="middle",
-            )(previous, gains, scale, series, factors, *middle_tables, *states),
+            )(previous[part], gains, scale, series, factors, forward, *middle_tables, *states),
         )
     (states,) = states
 
@@ -498,13 +552,12 @@
         last_kernel,
         grid=(steps,),
         in_specs=[VMEM] * 5,
-        out_specs=blocks(length),
+        out_specs=pl.BlockSpec((length, BLOCK), lambda i: (0, i)),
         out_shape=pltpu.HBM((length, channels), jnp.float32),
-        scratch_shapes=[vmem(BLOCK // LANES, length, LANES)],
-        compiler_params=params(16),
+        compiler_params=params(12),
         cost_estimate=cost(work),
         name="last",
-    )(states, gains, factors, sent, before)
+    )(states, gains, powers, sent, before)
 
 
 def solution(mesh):

time: 43.7 us -> 43.4 us (level)
  starting transfers between devices: 7.28 us -> 10.2 us
  waiting for transfers between devices: 13.4 us -> 11.1 us
  Pallas kernels: 22.8 us -> 21.9 us
    ppermute x4, waiting for transfers between devices: 13.4 us -> 9.47 us  [shards(): got = lax.ppermute(sent, 'tm', [(i, i ^ step) for i in range(count)])]
    ppermute x4, starting transfers between devices: 1.83 us -> 4.63 us  [shards(): got = lax.ppermute(sent, 'tm', [(i, i ^ step) for i in range(count)])]
    ppermute x1 -> x3, waiting for transfers between devices: 0.01 us -> 1.58 us  [shards(): previous.append(lax.ppermute(parts[part], 'tm', ahead))]
    pallas_call x1, Pallas kernels: 2.76 us -> 2.25 us  [shards(): pl.pallas_call(last_kernel, grid=(steps,), in_specs=[VMEM] * 5, out_specs...]
    pallas_call x3 -> x5, Pallas kernels: 18.3 us -> 17.9 us  [the longest x1 7.9 us: shards(): pl.pallas_call(own_kernel, grid=(steps,), in_specs=[HBM] * 2 + [VMEM] * 9...]
  transfers between devices with their start and end apart: 6 -> 8, of which waited for: 4 -> 5; matrix products, arithmetic and copies ran while one was open for 0% -> 0% of each run, Pallas kernels for 29% -> 35%
where the time goes in v1:
time: 43.4 us; the launch traced here: 43.3 us
  Pallas kernels  21.9 us (50%)
  waiting for transfers between devices  11.1 us (26%)
  starting transfers between devices  10.2 us (24%)
    ppermute x4, waiting for transfers between devices, shards(): got = lax.ppermute(sent, 'tm', [(i, i ^ step) for i in range(count)])  9.47 us
    pallas_call x1, Pallas kernels, shards(): pl.pallas_call(own_kernel, grid=(steps,), in_specs=[HBM] * 2 + [VMEM] * 9...  7.9 us
    pallas_call x3, Pallas kernels, shards(): pl.pallas_call(functools.partial(middle_kernel, first), grid=(end - first...  7.18 us
    ppermute x1, starting transfers between devices, shards(): following = lax.ppermute(sudden_shrink, 'tm', back)  5.03 us
    ppermute x4, starting transfers between devices, shards(): got = lax.ppermute(sent, 'tm', [(i, i ^ step) for i in range(count)])  4.63 us
    pallas_call x1, Pallas kernels, shards(): pl.pallas_call(load_kernel, in_specs=[HBM] * 11, out_specs=[VMEM] * 14, o...  2.81 us
    pallas_call x1, Pallas kernels, shards(): pl.pallas_call(last_kernel, grid=(steps,), in_specs=[VMEM] * 5, out_specs...  2.25 us
    ppermute x3, waiting for transfers between devices, shards(): previous.append(lax.ppermute(parts[part], 'tm', ahead))  1.58 us
  transfers between devices with their start and end apart: 8, of which 5 were waited for; matrix products, arithmetic and copies ran while one was open for 0% of the time, Pallas kernels for 35%

profile of v1, /device:TPU:0, one launch (start us, length us, event | category | flops | bytes accessed | tf_op | source)
XLA Modules:
  0.0 43.3 jit_solution(3766524772362669631)
XLA Ops:
  0.0 0.0 copy-start
  0.0 2.8 %load.1 = (bf16[384,1024]{1,0:T(8,128)(2,1)S(1)}, bf16[384,512]{1,0:T(8,128)(2,1)S(1)}, bf16[384,512]{1,0:T(8,128)(2,1)S(1)}, f32[4,768,128]{2,1,0:T(8,128)S(1)}...) custom-call(bf16[384,2048]{1,0:T(8,128)(2,1)} %section_hbm.3, ...), custom_call_target="tpu_custom_call" | custom-call | flops 150994944 | bytes 16777216 | tf_op jit(solution)/shard_map/load/pallas_call | solution.py:458
  2.8 0.5 %collective-permute-start.2 = (bf16[384,1024]{1,0:T(8,128)(2,1)S(1)}, bf16[384,1024]{1,0:T(8,128)(2,1)S(1)}, u32[]{:S(2)}, u32[]{:S(2)}) collective-permute-start(bf16[384,1024]{1,0:T(8,128)(2,1)S(1)} %get-tuple-element.35.part_ref), channel_id=1, source_target_pairs={{0,2},{2,4},{4,6},{6,8},{8,10},{10,12},{12,14},{14,16},{16,18},{18... | collective-permute-start | bytes 2359304 | tf_op jit(solution)/shard_map/ppermute | solution.py:480
  3.4 0.0 copy-done
  3.4 5.0 %collective-permute-start.3 = (f32[384]{0:T(512)S(1)}, f32[384]{0:T(512)S(1)}, u32[]{:S(2)}, u32[]{:S(2)}) collective-permute-start(f32[384]{0:T(512)S(1)} %copy-done), channel_id=1, source_target_pairs={{2,0},{4,2},{6,4},{8,6},{10,8},{12,10},{14,12},{16,14},{18,16},{20... | collective-permute-start | bytes 4616 | tf_op jit(solution)/shard_map/ppermute | solution.py:481
  8.4 0.0 collective-permute-start.1
  8.4 7.9 %own.1 = (f32[4,384,512]{2,1,0:T(8,128)S(1)}, f32[4,384,512]{2,1,0:T(8,128)S(1)}, f32[4,392,512]{2,1,0:T(8,128)S(1)}, f32[1,2048]{1,0:T(1,128)S(1)}, bf16[200,12...) custom-call(bf16[384,2048]{1,0:T(8,128)(2,1)} %section_hbm.3, f32[768,2048]{1,0:T(8,128)} %table_hbm.3, ...), custom_call_target="tpu_custom_call" | custom-call | flops 4227858432 | bytes 16777216 | tf_op jit(solution)/shard_map/own/pallas_call | solution.py:483
  16.3 0.0 collective-permute-done.3.burst_ref
  16.3 1.6 %next.1.sent_ref = f32[4,2048]{1,0:T(4,128)S(1)} custom-call(f32[4,384,512]{2,1,0:T(8,128)S(1)} %get-tuple-element.49.after_ref, f32[1,2048]{1,0:T(1,128)S(1)} %get-tuple-element.50.ends_ref, f32[8,2048]{1,0:T(8,128)S(1)} %get-tuple-element.34.gains_ref, f32[384]{0:T(512)S(1)} %collective-permute-done.3.burst_ref, f32[8,384]{1,0:T(8,128)S(1)} %get-tuple-element.51.rows_ref, ...), custom_call_target="tpu_custom_call" | custom-call | flops 603979776 | bytes 16777216 | tf_op jit(solution)/shard_map/next/pallas_call | solution.py:505
  17.9 0.1 collective-permute-start.4
  18.0 1.2 %collective-permute-done.4.got_ref = f32[4,2048]{1,0:T(4,128)S(1)} collective-permute-done((f32[4,2048]{1,0:T(4,128)S(1)}, f32[4,2048]{1,0:T(4,128)S(1)}, u32[]{:S(2)}, u32[]{:S(2)}) %collective-permute-start.4) | collective-permute-done | bytes 32800 | tf_op jit(solution)/shard_map/ppermute | solution.py:538
  19.2 1.5 %collective-permute-start.5 = (f32[4,2048]{1,0:T(4,128)S(1)}, f32[4,2048]{1,0:T(4,128)S(1)}, u32[]{:S(2)}, u32[]{:S(2)}) collective-permute-start(f32[4,2048]{1,0:T(4,128)S(1)} %get-tuple-element.53.sent_ref), channel_id=1, source_target_pairs={{0,4},{2,6},{4,0},{6,2},{8,12},{10,14},{12,8},{14,10},{16,20},{18,... | collective-permute-start | bytes 98312 | tf_op jit(solution)/shard_map/ppermute | solution.py:538
  20.7 2.5 %collective-permute-done.5.got_ref = f32[4,2048]{1,0:T(4,128)S(1)} collective-permute-done((f32[4,2048]{1,0:T(4,128)S(1)}, f32[4,2048]{1,0:T(4,128)S(1)}, u32[]{:S(2)}, u32[]{:S(2)}) %collective-permute-start.5) | collective-permute-done | bytes 32800 | tf_op jit(solution)/shard_map/ppermute | solution.py:538
  23.2 1.0 %collective-permute-start.6 = (f32[4,2048]{1,0:T(4,128)S(1)}, f32[4,2048]{1,0:T(4,128)S(1)}, u32[]{:S(2)}, u32[]{:S(2)}) collective-permute-start(f32[4,2048]{1,0:T(4,128)S(1)} %get-tuple-element.55.sent_ref), channel_id=1, source_target_pairs={{0,8},{2,10},{4,12},{6,14},{8,0},{10,2},{12,4},{14,6},{16,24},{18,... | collective-permute-start | bytes 98312 | tf_op jit(solution)/shard_map/ppermute | solution.py:538
  24.3 2.9 %collective-permute-done.6.got_ref = f32[4,2048]{1,0:T(4,128)S(1)} collective-permute-done((f32[4,2048]{1,0:T(4,128)S(1)}, f32[4,2048]{1,0:T(4,128)S(1)}, u32[]{:S(2)}, u32[]{:S(2)}) %collective-permute-start.6) | collective-permute-done | bytes 32800 | tf_op jit(solution)/shard_map/ppermute | solution.py:538
  27.3 2.0 %collective-permute-start.7 = (f32[4,2048]{1,0:T(4,128)S(1)}, f32[4,2048]{1,0:T(4,128)S(1)}, u32[]{:S(2)}, u32[]{:S(2)}) collective-permute-start(f32[4,2048]{1,0:T(4,128)S(1)} %get-tuple-element.57.sent_ref), channel_id=1, source_target_pairs={{0,16},{2,18},{4,20},{6,22},{8,24},{10,26},{12,28},{14,30},{16,0},... | collective-permute-start | bytes 98312 | tf_op jit(solution)/shard_map/ppermute | solution.py:538
  29.3 0.0 collective-permute-start
  29.3 2.8 %collective-permute-done.7.got_ref = f32[4,2048]{1,0:T(4,128)S(1)} collective-permute-done((f32[4,2048]{1,0:T(4,128)S(1)}, f32[4,2048]{1,0:T(4,128)S(1)}, u32[]{:S(2)}, u32[]{:S(2)}) %collective-permute-start.7) | collective-permute-done | bytes 32800 | tf_op jit(solution)/shard_map/ppermute | solution.py:538
  32.2 0.0 collective-permute-done.2.section_ref
  32.2 3.6 %middle.3.refs_0_ = f32[16,384,128]{2,1,0:T(8,128)S(1)} custom-call(bf16[384,1024]{1,0:T(8,128)(2,1)S(1)} %collective-permute-done.2.section_ref, f32[8,2048]{1,0:T(8,128)S(1)} %get-tuple-element.34.gains_ref, f32[4,392,512]{2,1,0:T(8,128)S(1)} %get-tuple-element.43.scale_ref, f32[4,384,512]{2,1,0:T(8,128)S(1)} %get-tuple-element.44.series_ref, ...), custom_call_target="tpu_custom_call" | custom-call | flops 2415919104 | bytes 16777216 | tf_op jit(solution)/shard_map/middle/pallas_call | solution.py:520
  35.8 0.0 collective-permute-done.1.section_ref
  35.8 1.8 %middle.4.refs_0_ = f32[16,384,128]{2,1,0:T(8,128)S(1)} custom-call(bf16[384,512]{1,0:T(8,128)(2,1)S(1)} %collective-permute-done.1.section_ref, f32[8,2048]{1,0:T(8,128)S(1)} %get-tuple-element.34.gains_ref, f32[4,392,512]{2,1,0:T(8,128)S(1)} %get-tuple-element.43.scale_ref, ...), custom_call_target="tpu_custom_call", output_to_operand_aliasing={{}: (8, {})} | custom-call | flops 2415919104 | bytes 16777216 | tf_op jit(solution)/shard_map/middle/pallas_call | solution.py:520
  37.6 1.6 %collective-permute-done.section_ref = bf16[384,512]{1,0:T(8,128)(2,1)S(1)} collective-permute-done((bf16[384,512]{1,0:T(8,128)(2,1)S(1)}, bf16[384,512]{1,0:T(8,128)(2,1)S(1)}, u32[]{:S(2)}, u32[]{:S(2)}) %collective-permute-start) | collective-permute-done | bytes 393248 | tf_op jit(solution)/shard_map/ppermute | solution.py:480
  39.2 1.8 %middle.5.states_ref = f32[16,384,128]{2,1,0:T(8,128)S(1)} custom-call(bf16[384,512]{1,0:T(8,128)(2,1)S(1)} %collective-permute-done.section_ref, f32[8,2048]{1,0:T(8,128)S(1)} %get-tuple-element.34.gains_ref, f32[4,392,512]{2,1,0:T(8,128)S(1)} %get-tuple-element.43.scale_ref, ...), custom_call_target="tpu_custom_call", output_to_operand_aliasing={{}: (8, {})} | custom-call | flops 2415919104 | bytes 16777216 | tf_op jit(solution)/shard_map/middle/pallas_call | solution.py:520
  41.0 2.3 %last.1 = f32[384,2048]{1,0:T(8,128)} custom-call(f32[16,384,128]{2,1,0:T(8,128)S(1)} %middle.5.states_ref, f32[8,2048]{1,0:T(8,128)S(1)} %get-tuple-element.34.gains_ref, f32[384,128]{1,0:T(8,128)S(1)} %get-tuple-element.48.powers_ref, f32[4,2048]{1,0:T(4,128)S(1)} %get-tuple-element.59.sent_ref, f32[3,2048]{1,0:T(4,128)S(1)} %get-tuple-element.60.before_ref), custom_call_target="tpu_custom_call" | custom-call | flops 603979776 | bytes 16777216 | tf_op jit(solution)/shard_map/last/pallas_call | solution.py:551
  (4 shorter events, 0.2 us)
Async XLA Ops:
  0.0 3.4 %copy-start = (f32[384]{0:T(512)S(1)}, f32[384]{0:T(512)}, u32[]{:S(2)}) copy-start(f32[384]{0:T(512)} %burst_hbm.1) | copy-start | bytes 4612
  2.8 29.4 %collective-permute-start.2 = (bf16[384,1024]{1,0:T(8,128)(2,1)S(1)}, bf16[384,1024]{1,0:T(8,128)(2,1)S(1)}, u32[]{:S(2)}, u32[]{:S(2)}) collective-permute-start(bf16[384,1024]{1,0:T(8,128)(2,1)S(1)} %get-tuple-element.35.part_ref), channel_id=1, source_target_pairs={{0,2},{2,4},{4,6},{6,8},{8,10},{10,12},{12,14},{14,16},{16,18},{18... | collective-permute-start | bytes 2359304 | tf_op jit(solution)/shard_map/ppermute | solution.py:480
  3.4 12.9 %collective-permute-start.3 = (f32[384]{0:T(512)S(1)}, f32[384]{0:T(512)S(1)}, u32[]{:S(2)}, u32[]{:S(2)}) collective-permute-start(f32[384]{0:T(512)S(1)} %copy-done), channel_id=1, source_target_pairs={{2,0},{4,2},{6,4},{8,6},{10,8},{12,10},{14,12},{16,14},{18,16},{20... | collective-permute-start | bytes 4616 | tf_op jit(solution)/shard_map/ppermute | solution.py:481
  8.4 27.4 %collective-permute-start.1 = (bf16[384,512]{1,0:T(8,128)(2,1)S(1)}, bf16[384,512]{1,0:T(8,128)(2,1)S(1)}, u32[]{:S(2)}, u32[]{:S(2)}) collective-permute-start(bf16[384,512]{1,0:T(8,128)(2,1)S(1)} %get-tuple-element.47), channel_id=1, source_target_pairs={{0,2},{2,4},{4,6},{6,8},{8,10},{10,12},{12,14},{14,16},{16,18},{18... | collective-permute-start | bytes 1179656 | tf_op jit(solution)/shard_map/ppermute | solution.py:480
  17.9 1.3 %collective-permute-start.4 = (f32[4,2048]{1,0:T(4,128)S(1)}, f32[4,2048]{1,0:T(4,128)S(1)}, u32[]{:S(2)}, u32[]{:S(2)}) collective-permute-start(f32[4,2048]{1,0:T(4,128)S(1)} %next.1.sent_ref), channel_id=1, source_target_pairs={{0,2},{2,0},{4,6},{6,4},{8,10},{10,8},{12,14},{14,12},{16,18},{18,... | collective-permute-start | bytes 98312 | tf_op jit(solution)/shard_map/ppermute | solution.py:538
  19.2 4.0 %collective-permute-start.5 = (f32[4,2048]{1,0:T(4,128)S(1)}, f32[4,2048]{1,0:T(4,128)S(1)}, u32[]{:S(2)}, u32[]{:S(2)}) collective-permute-start(f32[4,2048]{1,0:T(4,128)S(1)} %get-tuple-element.53.sent_ref), channel_id=1, source_target_pairs={{0,4},{2,6},{4,0},{6,2},{8,12},{10,14},{12,8},{14,10},{16,20},{18,... | collective-permute-start | bytes 98312 | tf_op jit(solution)/shard_map/ppermute | solution.py:538
  23.2 4.0 %collective-permute-start.6 = (f32[4,2048]{1,0:T(4,128)S(1)}, f32[4,2048]{1,0:T(4,128)S(1)}, u32[]{:S(2)}, u32[]{:S(2)}) collective-permute-start(f32[4,2048]{1,0:T(4,128)S(1)} %get-tuple-element.55.sent_ref), channel_id=1, source_target_pairs={{0,8},{2,10},{4,12},{6,14},{8,0},{10,2},{12,4},{14,6},{16,24},{18,... | collective-permute-start | bytes 98312 | tf_op jit(solution)/shard_map/ppermute | solution.py:538
  27.3 4.9 %collective-permute-start.7 = (f32[4,2048]{1,0:T(4,128)S(1)}, f32[4,2048]{1,0:T(4,128)S(1)}, u32[]{:S(2)}, u32[]{:S(2)}) collective-permute-start(f32[4,2048]{1,0:T(4,128)S(1)} %get-tuple-element.57.sent_ref), channel_id=1, source_target_pairs={{0,16},{2,18},{4,20},{6,22},{8,24},{10,26},{12,28},{14,30},{16,0},... | collective-permute-start | bytes 98312 | tf_op jit(solution)/shard_map/ppermute | solution.py:538
  29.3 9.9 %collective-permute-start = (bf16[384,512]{1,0:T(8,128)(2,1)S(1)}, bf16[384,512]{1,0:T(8,128)(2,1)S(1)}, u32[]{:S(2)}, u32[]{:S(2)}) collective-permute-start(bf16[384,512]{1,0:T(8,128)(2,1)S(1)} %get-tuple-element.33), channel_id=1, source_target_pairs={{0,2},{2,4},{4,6},{6,8},{8,10},{10,12},{12,14},{14,16},{16,18},{18... | collective-permute-start | bytes 1179656 | tf_op jit(solution)/shard_map/ppermute | solution.py:480

commit v2 on v1

--- a/solution.py
+++ b/solution.py
@@ -12,6 +12,7 @@
 SEGMENTS = 8
 BLOCK = 512
 NYQUIST_ROWS = 16
+OUT_BLOCK = 1024
 
 
 def split(table):
@@ -344,7 +345,7 @@
 
 
 def middle_kernel(
-    first, section_ref, gains_ref, scale_ref, series_ref, factors_ref, forward_ref, sums_ref,
+    first, begin, section_ref, gains_ref, scale_ref, series_ref, factors_ref, forward_ref, sums_ref,
     differences_ref, *refs,
 ):
     *_, states_ref, work_ref = refs
@@ -355,7 +356,7 @@
     half = length // 2
     segment = half // SEGMENTS
     even_cos, even_sin, odd_cos, odd_sin = spectra(
-        section_ref[:, columns_of(step - first)],
+        section_ref[:, columns_of(step - begin)],
         scale_ref[pl.ds(0, half), :],
         scale_ref[pl.ds(length, 1), :],
         scale_ref[pl.ds(half, half), :],
@@ -392,8 +393,8 @@
 
 def last_kernel(states_ref, gains_ref, powers_ref, sent_ref, before_ref, out_ref):
     step = pl.program_id(0)
-    at = columns_of(step)
     length, columns = out_ref.shape
+    at = pl.ds(pl.multiple_of(step * columns, columns), columns)
     keep = gains_ref[pl.ds(0, 1), at]
     state, spill, total, later = (sent_ref[pl.ds(row, 1), at] for row in range(4))
     before, decay, decay_later = (before_ref[pl.ds(row, 1), at] for row in range(3))
@@ -515,10 +516,14 @@
     )(after, ends, gains, following, rows, places)
 
     states = ()
-    for part, (first, end) in enumerate(zip(cuts, cuts[1:])):
+    pieces = (
+        (0, cuts[1] // 2, 0, 0), (cuts[1] // 2, cuts[1], 0, 0),
+        (cuts[1], cuts[2], 1, cuts[1]), (cuts[2], cuts[3], 2, cuts[2]),
+    )
+    for first, end, source, begin in pieces:
         states = (
             pl.pallas_call(
-                functools.partial(middle_kernel, first),
+                functools.partial(middle_kernel, first, begin),
                 grid=(end - first,),
                 in_specs=[VMEM] * (8 + len(states)),
                 out_specs=VMEM,
@@ -528,7 +533,7 @@
                 compiler_params=params(24),
                 cost_estimate=cost(4 * work),
                 name="middle",
-            )(previous[part], gains, scale, series, factors, forward, *middle_tables, *states),
+            )(previous[source], gains, scale, series, factors, forward, *middle_tables, *states),
         )
     (states,) = states
 
@@ -550,9 +555,9 @@
 
     return pl.pallas_call(
         last_kernel,
-        grid=(steps,),
+        grid=(channels // OUT_BLOCK,),
         in_specs=[VMEM] * 5,
-        out_specs=pl.BlockSpec((length, BLOCK), lambda i: (0, i)),
+        out_specs=pl.BlockSpec((length, OUT_BLOCK), lambda i: (0, i)),
         out_shape=pltpu.HBM((length, channels), jnp.float32),
         compiler_params=params(12),
         cost_estimate=cost(work),

time: 43.4 us -> 46.4 us (1.069)
  waiting for transfers between devices: 11.1 us -> 16.8 us
  starting transfers between devices: 10.2 us -> 7.92 us
    ppermute x3, waiting for transfers between devices: 1.58 us -> 5.05 us  [shards(): previous.append(lax.ppermute(parts[part], 'tm', ahead))]
    ppermute x4, starting transfers between devices: 4.63 us -> 1.64 us  [shards(): got = lax.ppermute(sent, 'tm', [(i, i ^ step) for i in range(count)])]
    ppermute x4, waiting for transfers between devices: 9.47 us -> 11.7 us  [shards(): got = lax.ppermute(sent, 'tm', [(i, i ^ step) for i in range(count)])]
    ppermute x3, starting transfers between devices: 0.55 us -> 1.26 us  [shards(): previous.append(lax.ppermute(parts[part], 'tm', ahead))]
    pallas_call x4 -> x5, Pallas kernels: 9.44 us -> 9.03 us  [the longest x4 7.14 us: shards(): pl.pallas_call(functools.partial(middle_kernel, first, begin), grid=(end...]
  transfers between devices with their start and end apart: 8 -> 8, of which waited for: 5 -> 6; matrix products, arithmetic and copies ran while one was open for 0% -> 0% of each run, Pallas kernels for 35% -> 32%
where the time goes in v2:
time: 46.4 us; the launch traced here: 46.3 us
  Pallas kernels  21.5 us (46%)
  waiting for transfers between devices  16.8 us (36%)
  starting transfers between devices  7.92 us (17%)
    ppermute x4, waiting for transfers between devices, shards(): got = lax.ppermute(sent, 'tm', [(i, i ^ step) for i in range(count)])  11.7 us
    pallas_call x1, Pallas kernels, shards(): pl.pallas_call(own_kernel, grid=(steps,), in_specs=[HBM] * 2 + [VMEM] * 9...  7.89 us
    pallas_call x4, Pallas kernels, shards(): pl.pallas_call(functools.partial(middle_kernel, first, begin), grid=(end...  7.14 us
    ppermute x3, waiting for transfers between devices, shards(): previous.append(lax.ppermute(parts[part], 'tm', ahead))  5.05 us
    ppermute x1, starting transfers between devices, shards(): following = lax.ppermute(sudden_shrink, 'tm', back)  5.03 us
    pallas_call x1, Pallas kernels, shards(): pl.pallas_call(load_kernel, in_specs=[HBM] * 11, out_specs=[VMEM] * 14, o...  2.81 us
    pallas_call x1, Pallas kernels, shards(): pl.pallas_call(last_kernel, grid=(channels // OUT_BLOCK,), in_specs=[VMEM...  1.89 us
    ppermute x4, starting transfers between devices, shards(): got = lax.ppermute(sent, 'tm', [(i, i ^ step) for i in range(count)])  1.64 us
  transfers between devices with their start and end apart: 8, of which 6 were waited for; matrix products, arithmetic and copies ran while one was open for 0% of the time, Pallas kernels for 32%

profile of v2, /device:TPU:0, one launch (start us, length us, event | category | flops | bytes accessed | tf_op | source)
XLA Modules:
  0.0 46.3 jit_solution(11110034396388211736)
XLA Ops:
  0.0 0.0 copy-start
  0.0 2.8 %load.1 = (bf16[384,1024]{1,0:T(8,128)(2,1)S(1)}, bf16[384,512]{1,0:T(8,128)(2,1)S(1)}, bf16[384,512]{1,0:T(8,128)(2,1)S(1)}, f32[4,768,128]{2,1,0:T(8,128)S(1)}...) custom-call(bf16[384,2048]{1,0:T(8,128)(2,1)} %section_hbm.3, ...), custom_call_target="tpu_custom_call" | custom-call | flops 150994944 | bytes 16777216 | tf_op jit(solution)/shard_map/load/pallas_call | solution.py:459
  2.8 0.5 %collective-permute-start.2 = (bf16[384,1024]{1,0:T(8,128)(2,1)S(1)}, bf16[384,1024]{1,0:T(8,128)(2,1)S(1)}, u32[]{:S(2)}, u32[]{:S(2)}) collective-permute-start(bf16[384,1024]{1,0:T(8,128)(2,1)S(1)} %get-tuple-element.35.part_ref), channel_id=1, source_target_pairs={{0,2},{2,4},{4,6},{6,8},{8,10},{10,12},{12,14},{14,16},{16,18},{18... | collective-permute-start | bytes 2359304 | tf_op jit(solution)/shard_map/ppermute | solution.py:481
  3.4 0.0 copy-done
  3.4 5.0 %collective-permute-start.3 = (f32[384]{0:T(512)S(1)}, f32[384]{0:T(512)S(1)}, u32[]{:S(2)}, u32[]{:S(2)}) collective-permute-start(f32[384]{0:T(512)S(1)} %copy-done), channel_id=1, source_target_pairs={{2,0},{4,2},{6,4},{8,6},{10,8},{12,10},{14,12},{16,14},{18,16},{20... | collective-permute-start | bytes 4616 | tf_op jit(solution)/shard_map/ppermute | solution.py:482
  8.4 7.9 %own.1 = (f32[4,384,512]{2,1,0:T(8,128)S(1)}, f32[4,384,512]{2,1,0:T(8,128)S(1)}, f32[4,392,512]{2,1,0:T(8,128)S(1)}, f32[1,2048]{1,0:T(1,128)S(1)}, bf16[200,12...) custom-call(bf16[384,2048]{1,0:T(8,128)(2,1)} %section_hbm.3, f32[768,2048]{1,0:T(8,128)} %table_hbm.3, ...), custom_call_target="tpu_custom_call" | custom-call | flops 4227858432 | bytes 16777216 | tf_op jit(solution)/shard_map/own/pallas_call | solution.py:484
  16.3 0.0 collective-permute-done.3.burst_ref
  16.3 1.6 %next.1.sent_ref = f32[4,2048]{1,0:T(4,128)S(1)} custom-call(f32[4,384,512]{2,1,0:T(8,128)S(1)} %get-tuple-element.49.after_ref, f32[1,2048]{1,0:T(1,128)S(1)} %get-tuple-element.50.ends_ref, f32[8,2048]{1,0:T(8,128)S(1)} %get-tuple-element.34.gains_ref, f32[384]{0:T(512)S(1)} %collective-permute-done.3.burst_ref, f32[8,384]{1,0:T(8,128)S(1)} %get-tuple-element.51.rows_ref, ...), custom_call_target="tpu_custom_call" | custom-call | flops 603979776 | bytes 16777216 | tf_op jit(solution)/shard_map/next/pallas_call | solution.py:506
  17.9 0.1 collective-permute-start.4
  18.0 1.2 %collective-permute-done.4.got_ref = f32[4,2048]{1,0:T(4,128)S(1)} collective-permute-done((f32[4,2048]{1,0:T(4,128)S(1)}, f32[4,2048]{1,0:T(4,128)S(1)}, u32[]{:S(2)}, u32[]{:S(2)}) %collective-permute-start.4) | collective-permute-done | bytes 32800 | tf_op jit(solution)/shard_map/ppermute | solution.py:543
  19.2 0.1 collective-permute-start.5
  19.3 3.9 %collective-permute-done.5.got_ref = f32[4,2048]{1,0:T(4,128)S(1)} collective-permute-done((f32[4,2048]{1,0:T(4,128)S(1)}, f32[4,2048]{1,0:T(4,128)S(1)}, u32[]{:S(2)}, u32[]{:S(2)}) %collective-permute-start.5) | collective-permute-done | bytes 32800 | tf_op jit(solution)/shard_map/ppermute | solution.py:543
  23.2 0.2 collective-permute-start.6
  23.5 3.7 %collective-permute-done.6.got_ref = f32[4,2048]{1,0:T(4,128)S(1)} collective-permute-done((f32[4,2048]{1,0:T(4,128)S(1)}, f32[4,2048]{1,0:T(4,128)S(1)}, u32[]{:S(2)}, u32[]{:S(2)}) %collective-permute-start.6) | collective-permute-done | bytes 32800 | tf_op jit(solution)/shard_map/ppermute | solution.py:543
  27.3 1.3 %collective-permute-start.7 = (f32[4,2048]{1,0:T(4,128)S(1)}, f32[4,2048]{1,0:T(4,128)S(1)}, u32[]{:S(2)}, u32[]{:S(2)}) collective-permute-start(f32[4,2048]{1,0:T(4,128)S(1)} %get-tuple-element.57.sent_ref), channel_id=1, source_target_pairs={{0,16},{2,18},{4,20},{6,22},{8,24},{10,26},{12,28},{14,30},{16,0},... | collective-permute-start | bytes 98312 | tf_op jit(solution)/shard_map/ppermute | solution.py:543
  28.5 0.0 collective-permute-start.1
  28.5 0.7 %collective-permute-start = (bf16[384,512]{1,0:T(8,128)(2,1)S(1)}, bf16[384,512]{1,0:T(8,128)(2,1)S(1)}, u32[]{:S(2)}, u32[]{:S(2)}) collective-permute-start(bf16[384,512]{1,0:T(8,128)(2,1)S(1)} %get-tuple-element.33), channel_id=1, source_target_pairs={{0,2},{2,4},{4,6},{6,8},{8,10},{10,12},{12,14},{14,16},{16,18},{18... | collective-permute-start | bytes 1179656 | tf_op jit(solution)/shard_map/ppermute | solution.py:481
  29.2 2.9 %collective-permute-done.7.got_ref = f32[4,2048]{1,0:T(4,128)S(1)} collective-permute-done((f32[4,2048]{1,0:T(4,128)S(1)}, f32[4,2048]{1,0:T(4,128)S(1)}, u32[]{:S(2)}, u32[]{:S(2)}) %collective-permute-start.7) | collective-permute-done | bytes 32800 | tf_op jit(solution)/shard_map/ppermute | solution.py:543
  32.2 0.0 collective-permute-done.2.section_ref
  32.2 1.8 %middle.4.refs_0_ = f32[16,384,128]{2,1,0:T(8,128)S(1)} custom-call(bf16[384,1024]{1,0:T(8,128)(2,1)S(1)} %collective-permute-done.2.section_ref, f32[8,2048]{1,0:T(8,128)S(1)} %get-tuple-element.34.gains_ref, f32[4,392,512]{2,1,0:T(8,128)S(1)} %get-tuple-element.43.scale_ref, f32[4,384,512]{2,1,0:T(8,128)S(1)} %get-tuple-element.44.series_ref, ...), custom_call_target="tpu_custom_call" | custom-call | flops 2415919104 | bytes 16777216 | tf_op jit(solution)/shard_map/middle/pallas_call | solution.py:525
  34.0 1.8 %middle.5.refs_0_ = f32[16,384,128]{2,1,0:T(8,128)S(1)} custom-call(bf16[384,1024]{1,0:T(8,128)(2,1)S(1)} %collective-permute-done.2.section_ref, f32[8,2048]{1,0:T(8,128)S(1)} %get-tuple-element.34.gains_ref, f32[4,392,512]{2,1,0:T(8,128)S(1)} %get-tuple-element.43.scale_ref, ...), custom_call_target="tpu_custom_call", output_to_operand_aliasing={{}: (8, {})} | custom-call | flops 2415919104 | bytes 16777216 | tf_op jit(solution)/shard_map/middle/pallas_call | solution.py:525
  35.8 2.6 %collective-permute-done.1.section_ref = bf16[384,512]{1,0:T(8,128)(2,1)S(1)} collective-permute-done((bf16[384,512]{1,0:T(8,128)(2,1)S(1)}, bf16[384,512]{1,0:T(8,128)(2,1)S(1)}, u32[]{:S(2)}, u32[]{:S(2)}) %collective-permute-start.1) | collective-permute-done | bytes 393248 | tf_op jit(solution)/shard_map/ppermute | solution.py:481
  38.4 1.8 %middle.6.refs_0_ = f32[16,384,128]{2,1,0:T(8,128)S(1)} custom-call(bf16[384,512]{1,0:T(8,128)(2,1)S(1)} %collective-permute-done.1.section_ref, f32[8,2048]{1,0:T(8,128)S(1)} %get-tuple-element.34.gains_ref, f32[4,392,512]{2,1,0:T(8,128)S(1)} %get-tuple-element.43.scale_ref, ...), custom_call_target="tpu_custom_call", output_to_operand_aliasing={{}: (8, {})} | custom-call | flops 2415919104 | bytes 16777216 | tf_op jit(solution)/shard_map/middle/pallas_call | solution.py:525
  40.2 2.4 %collective-permute-done.section_ref = bf16[384,512]{1,0:T(8,128)(2,1)S(1)} collective-permute-done((bf16[384,512]{1,0:T(8,128)(2,1)S(1)}, bf16[384,512]{1,0:T(8,128)(2,1)S(1)}, u32[]{:S(2)}, u32[]{:S(2)}) %collective-permute-start) | collective-permute-done | bytes 393248 | tf_op jit(solution)/shard_map/ppermute | solution.py:481
  42.6 1.8 %middle.7.states_ref = f32[16,384,128]{2,1,0:T(8,128)S(1)} custom-call(bf16[384,512]{1,0:T(8,128)(2,1)S(1)} %collective-permute-done.section_ref, f32[8,2048]{1,0:T(8,128)S(1)} %get-tuple-element.34.gains_ref, f32[4,392,512]{2,1,0:T(8,128)S(1)} %get-tuple-element.43.scale_ref, ...), custom_call_target="tpu_custom_call", output_to_operand_aliasing={{}: (8, {})} | custom-call | flops 2415919104 | bytes 16777216 | tf_op jit(solution)/shard_map/middle/pallas_call | solution.py:525
  44.4 1.9 %last.1 = f32[384,2048]{1,0:T(8,128)} custom-call(f32[16,384,128]{2,1,0:T(8,128)S(1)} %middle.7.states_ref, f32[8,2048]{1,0:T(8,128)S(1)} %get-tuple-element.34.gains_ref, f32[384,128]{1,0:T(8,128)S(1)} %get-tuple-element.48.powers_ref, f32[4,2048]{1,0:T(4,128)S(1)} %get-tuple-element.59.sent_ref, f32[3,2048]{1,0:T(4,128)S(1)} %get-tuple-element.60.before_ref), custom_call_target="tpu_custom_call" | custom-call | flops 603979776 | bytes 16777216 | tf_op jit(solution)/shard_map/last/pallas_call | solution.py:556
  (4 shorter events, 0.2 us)
Async XLA Ops:
  0.0 3.4 %copy-start = (f32[384]{0:T(512)S(1)}, f32[384]{0:T(512)}, u32[]{:S(2)}) copy-start(f32[384]{0:T(512)} %burst_hbm.1) | copy-start | bytes 4612
  2.8 29.4 %collective-permute-start.2 = (bf16[384,1024]{1,0:T(8,128)(2,1)S(1)}, bf16[384,1024]{1,0:T(8,128)(2,1)S(1)}, u32[]{:S(2)}, u32[]{:S(2)}) collective-permute-start(bf16[384,1024]{1,0:T(8,128)(2,1)S(1)} %get-tuple-element.35.part_ref), channel_id=1, source_target_pairs={{0,2},{2,4},{4,6},{6,8},{8,10},{10,12},{12,14},{14,16},{16,18},{18... | collective-permute-start | bytes 2359304 | tf_op jit(solution)/shard_map/ppermute | solution.py:481
  3.4 12.9 %collective-permute-start.3 = (f32[384]{0:T(512)S(1)}, f32[384]{0:T(512)S(1)}, u32[]{:S(2)}, u32[]{:S(2)}) collective-permute-start(f32[384]{0:T(512)S(1)} %copy-done), channel_id=1, source_target_pairs={{2,0},{4,2},{6,4},{8,6},{10,8},{12,10},{14,12},{16,14},{18,16},{20... | collective-permute-start | bytes 4616 | tf_op jit(solution)/shard_map/ppermute | solution.py:482
  17.9 1.3 %collective-permute-start.4 = (f32[4,2048]{1,0:T(4,128)S(1)}, f32[4,2048]{1,0:T(4,128)S(1)}, u32[]{:S(2)}, u32[]{:S(2)}) collective-permute-start(f32[4,2048]{1,0:T(4,128)S(1)} %next.1.sent_ref), channel_id=1, source_target_pairs={{0,2},{2,0},{4,6},{6,4},{8,10},{10,8},{12,14},{14,12},{16,18},{18,... | collective-permute-start | bytes 98312 | tf_op jit(solution)/shard_map/ppermute | solution.py:543
  19.2 4.0 %collective-permute-start.5 = (f32[4,2048]{1,0:T(4,128)S(1)}, f32[4,2048]{1,0:T(4,128)S(1)}, u32[]{:S(2)}, u32[]{:S(2)}) collective-permute-start(f32[4,2048]{1,0:T(4,128)S(1)} %get-tuple-element.53.sent_ref), channel_id=1, source_target_pairs={{0,4},{2,6},{4,0},{6,2},{8,12},{10,14},{12,8},{14,10},{16,20},{18,... | collective-permute-start | bytes 98312 | tf_op jit(solution)/shard_map/ppermute | solution.py:543
  23.2 4.0 %collective-permute-start.6 = (f32[4,2048]{1,0:T(4,128)S(1)}, f32[4,2048]{1,0:T(4,128)S(1)}, u32[]{:S(2)}, u32[]{:S(2)}) collective-permute-start(f32[4,2048]{1,0:T(4,128)S(1)} %get-tuple-element.55.sent_ref), channel_id=1, source_target_pairs={{0,8},{2,10},{4,12},{6,14},{8,0},{10,2},{12,4},{14,6},{16,24},{18,... | collective-permute-start | bytes 98312 | tf_op jit(solution)/shard_map/ppermute | solution.py:543
  27.3 4.9 %collective-permute-start.7 = (f32[4,2048]{1,0:T(4,128)S(1)}, f32[4,2048]{1,0:T(4,128)S(1)}, u32[]{:S(2)}, u32[]{:S(2)}) collective-permute-start(f32[4,2048]{1,0:T(4,128)S(1)} %get-tuple-element.57.sent_ref), channel_id=1, source_target_pairs={{0,16},{2,18},{4,20},{6,22},{8,24},{10,26},{12,28},{14,30},{16,0},... | collective-permute-start | bytes 98312 | tf_op jit(solution)/shard_map/ppermute | solution.py:543
  28.5 9.9 %collective-permute-start.1 = (bf16[384,512]{1,0:T(8,128)(2,1)S(1)}, bf16[384,512]{1,0:T(8,128)(2,1)S(1)}, u32[]{:S(2)}, u32[]{:S(2)}) collective-permute-start(bf16[384,512]{1,0:T(8,128)(2,1)S(1)} %get-tuple-element.47), channel_id=1, source_target_pairs={{0,2},{2,4},{4,6},{6,8},{8,10},{10,12},{12,14},{14,16},{16,18},{18... | collective-permute-start | bytes 1179656 | tf_op jit(solution)/shard_map/ppermute | solution.py:481
  28.5 14.1 %collective-permute-start = (bf16[384,512]{1,0:T(8,128)(2,1)S(1)}, bf16[384,512]{1,0:T(8,128)(2,1)S(1)}, u32[]{:S(2)}, u32[]{:S(2)}) collective-permute-start(bf16[384,512]{1,0:T(8,128)(2,1)S(1)} %get-tuple-element.33), channel_id=1, source_target_pairs={{0,2},{2,4},{4,6},{6,8},{8,10},{10,12},{12,14},{14,16},{16,18},{18... | collective-permute-start | bytes 1179656 | tf_op jit(solution)/shard_map/ppermute | solution.py:481

commit v3 on v2

--- a/solution.py
+++ b/solution.py
@@ -311,16 +311,15 @@
     def _():
         spread(burst_ref, rows_ref, blocks_ref, factors_ref)
 
-    after_ref = after_ref.at[step]
-    columns = after_ref.shape[1]
-    at = columns_of(step)
-    out_ref[pl.ds(0, 1), at] = ends_ref[pl.ds(0, 1), at]
-    out_ref[pl.ds(1, 1), at] = scan(
-        lambda block: after_ref[rows_of(block), :], factors_ref,
-        gains_ref[pl.ds(0, 1), at], gains_ref[pl.ds(1, 1), at],
-    )
-    out_ref[pl.ds(2, 1), at] = gains_ref[pl.ds(2, 1), at]
-    out_ref[pl.ds(3, 1), at] = jnp.ones((1, columns), jnp.float32)
+    for block in (2 * step, 2 * step + 1):
+        after, at = after_ref.at[block], columns_of(block)
+        out_ref[pl.ds(0, 1), at] = ends_ref[pl.ds(0, 1), at]
+        out_ref[pl.ds(1, 1), at] = scan(
+            lambda row, after=after: after[rows_of(row), :], factors_ref,
+            gains_ref[pl.ds(0, 1), at], gains_ref[pl.ds(1, 1), at],
+        )
+        out_ref[pl.ds(2, 1), at] = gains_ref[pl.ds(2, 1), at]
+        out_ref[pl.ds(3, 1), at] = jnp.ones((1, BLOCK), jnp.float32)
 
 
 def merge_kernel(step, sent_ref, got_ref, *refs):
@@ -505,7 +504,7 @@
 
     sent = pl.pallas_call(
         next_kernel,
-        grid=(steps,),
+        grid=(steps // 2,),
         in_specs=[VMEM] * 6,
         out_specs=VMEM,
         out_shape=vmem(4, channels),

time: 46.4 us -> 46.4 us (level)
  no operation moved by 1% of the time
where the time goes in v3:
time: 46.4 us; the launch traced here: 46.3 us
  Pallas kernels  21.4 us (46%)
  waiting for transfers between devices  16.8 us (36%)
  starting transfers between devices  7.92 us (17%)
    ppermute x4, waiting for transfers between devices, shards(): got = lax.ppermute(sent, 'tm', [(i, i ^ step) for i in range(count)])  11.7 us
    pallas_call x1, Pallas kernels, shards(): pl.pallas_call(own_kernel, grid=(steps,), in_specs=[HBM] * 2 + [VMEM] * 9...  7.89 us
    pallas_call x4, Pallas kernels, shards(): pl.pallas_call(functools.partial(middle_kernel, first, begin), grid=(end...  7.15 us
    ppermute x3, waiting for transfers between devices, shards(): previous.append(lax.ppermute(parts[part], 'tm', ahead))  5.05 us
    ppermute x1, starting transfers between devices, shards(): following = lax.ppermute(sudden_shrink, 'tm', back)  5.03 us
    pallas_call x1, Pallas kernels, shards(): pl.pallas_call(load_kernel, in_specs=[HBM] * 11, out_specs=[VMEM] * 14, o...  2.81 us
    pallas_call x1, Pallas kernels, shards(): pl.pallas_call(last_kernel, grid=(channels // OUT_BLOCK,), in_specs=[VMEM...  1.89 us
    ppermute x4, starting transfers between devices, shards(): got = lax.ppermute(sent, 'tm', [(i, i ^ step) for i in range(count)])  1.64 us
  transfers between devices with their start and end apart: 8, of which 6 were waited for; matrix products, arithmetic and copies ran while one was open for 0% of the time, Pallas kernels for 32%

profile of v3, /device:TPU:0, one launch (start us, length us, event | category | flops | bytes accessed | tf_op | source)
XLA Modules:
  0.0 46.3 jit_solution(15569610079853092053)
XLA Ops:
  0.0 0.0 copy-start
  0.0 2.8 %load.1 = (bf16[384,1024]{1,0:T(8,128)(2,1)S(1)}, bf16[384,512]{1,0:T(8,128)(2,1)S(1)}, bf16[384,512]{1,0:T(8,128)(2,1)S(1)}, f32[4,768,128]{2,1,0:T(8,128)S(1)}...) custom-call(bf16[384,2048]{1,0:T(8,128)(2,1)} %section_hbm.3, ...), custom_call_target="tpu_custom_call" | custom-call | flops 150994944 | bytes 16777216 | tf_op jit(solution)/shard_map/load/pallas_call | solution.py:458
  2.8 0.5 %collective-permute-start.2 = (bf16[384,1024]{1,0:T(8,128)(2,1)S(1)}, bf16[384,1024]{1,0:T(8,128)(2,1)S(1)}, u32[]{:S(2)}, u32[]{:S(2)}) collective-permute-start(bf16[384,1024]{1,0:T(8,128)(2,1)S(1)} %get-tuple-element.35.part_ref), channel_id=1, source_target_pairs={{0,2},{2,4},{4,6},{6,8},{8,10},{10,12},{12,14},{14,16},{16,18},{18... | collective-permute-start | bytes 2359304 | tf_op jit(solution)/shard_map/ppermute | solution.py:480
  3.4 0.0 copy-done
  3.4 5.0 %collective-permute-start.3 = (f32[384]{0:T(512)S(1)}, f32[384]{0:T(512)S(1)}, u32[]{:S(2)}, u32[]{:S(2)}) collective-permute-start(f32[384]{0:T(512)S(1)} %copy-done), channel_id=1, source_target_pairs={{2,0},{4,2},{6,4},{8,6},{10,8},{12,10},{14,12},{16,14},{18,16},{20... | collective-permute-start | bytes 4616 | tf_op jit(solution)/shard_map/ppermute | solution.py:481
  8.4 7.9 %own.1 = (f32[4,384,512]{2,1,0:T(8,128)S(1)}, f32[4,384,512]{2,1,0:T(8,128)S(1)}, f32[4,392,512]{2,1,0:T(8,128)S(1)}, f32[1,2048]{1,0:T(1,128)S(1)}, bf16[200,12...) custom-call(bf16[384,2048]{1,0:T(8,128)(2,1)} %section_hbm.3, f32[768,2048]{1,0:T(8,128)} %table_hbm.3, ...), custom_call_target="tpu_custom_call" | custom-call | flops 4227858432 | bytes 16777216 | tf_op jit(solution)/shard_map/own/pallas_call | solution.py:483
  16.3 0.0 collective-permute-done.3.burst_ref
  16.3 1.5 %next.1.sent_ref = f32[4,2048]{1,0:T(4,128)S(1)} custom-call(f32[4,384,512]{2,1,0:T(8,128)S(1)} %get-tuple-element.49.after_ref, f32[1,2048]{1,0:T(1,128)S(1)} %get-tuple-element.50.ends_ref, f32[8,2048]{1,0:T(8,128)S(1)} %get-tuple-element.34.gains_ref, f32[384]{0:T(512)S(1)} %collective-permute-done.3.burst_ref, f32[8,384]{1,0:T(8,128)S(1)} %get-tuple-element.51.rows_ref, ...), custom_call_target="tpu_custom_call" | custom-call | flops 603979776 | bytes 16777216 | tf_op jit(solution)/shard_map/next/pallas_call | solution.py:505
  17.8 0.1 collective-permute-start.4
  17.9 1.2 %collective-permute-done.4.got_ref = f32[4,2048]{1,0:T(4,128)S(1)} collective-permute-done((f32[4,2048]{1,0:T(4,128)S(1)}, f32[4,2048]{1,0:T(4,128)S(1)}, u32[]{:S(2)}, u32[]{:S(2)}) %collective-permute-start.4) | collective-permute-done | bytes 32800 | tf_op jit(solution)/shard_map/ppermute | solution.py:542
  19.1 0.1 collective-permute-start.5
  19.2 3.9 %collective-permute-done.5.got_ref = f32[4,2048]{1,0:T(4,128)S(1)} collective-permute-done((f32[4,2048]{1,0:T(4,128)S(1)}, f32[4,2048]{1,0:T(4,128)S(1)}, u32[]{:S(2)}, u32[]{:S(2)}) %collective-permute-start.5) | collective-permute-done | bytes 32800 | tf_op jit(solution)/shard_map/ppermute | solution.py:542
  23.2 0.2 collective-permute-start.6
  23.4 3.7 %collective-permute-done.6.got_ref = f32[4,2048]{1,0:T(4,128)S(1)} collective-permute-done((f32[4,2048]{1,0:T(4,128)S(1)}, f32[4,2048]{1,0:T(4,128)S(1)}, u32[]{:S(2)}, u32[]{:S(2)}) %collective-permute-start.6) | collective-permute-done | bytes 32800 | tf_op jit(solution)/shard_map/ppermute | solution.py:542
  27.2 1.3 %collective-permute-start.7 = (f32[4,2048]{1,0:T(4,128)S(1)}, f32[4,2048]{1,0:T(4,128)S(1)}, u32[]{:S(2)}, u32[]{:S(2)}) collective-permute-start(f32[4,2048]{1,0:T(4,128)S(1)} %get-tuple-element.57.sent_ref), channel_id=1, source_target_pairs={{0,16},{2,18},{4,20},{6,22},{8,24},{10,26},{12,28},{14,30},{16,0},... | collective-permute-start | bytes 98312 | tf_op jit(solution)/shard_map/ppermute | solution.py:542
  28.5 0.0 collective-permute-start.1
  28.5 0.7 %collective-permute-start = (bf16[384,512]{1,0:T(8,128)(2,1)S(1)}, bf16[384,512]{1,0:T(8,128)(2,1)S(1)}, u32[]{:S(2)}, u32[]{:S(2)}) collective-permute-start(bf16[384,512]{1,0:T(8,128)(2,1)S(1)} %get-tuple-element.33), channel_id=1, source_target_pairs={{0,2},{2,4},{4,6},{6,8},{8,10},{10,12},{12,14},{14,16},{16,18},{18... | collective-permute-start | bytes 1179656 | tf_op jit(solution)/shard_map/ppermute | solution.py:480
  29.2 2.9 %collective-permute-done.7.got_ref = f32[4,2048]{1,0:T(4,128)S(1)} collective-permute-done((f32[4,2048]{1,0:T(4,128)S(1)}, f32[4,2048]{1,0:T(4,128)S(1)}, u32[]{:S(2)}, u32[]{:S(2)}) %collective-permute-start.7) | collective-permute-done | bytes 32800 | tf_op jit(solution)/shard_map/ppermute | solution.py:542
  32.1 0.0 collective-permute-done.2.section_ref
  32.1 1.8 %middle.4.refs_0_ = f32[16,384,128]{2,1,0:T(8,128)S(1)} custom-call(bf16[384,1024]{1,0:T(8,128)(2,1)S(1)} %collective-permute-done.2.section_ref, f32[8,2048]{1,0:T(8,128)S(1)} %get-tuple-element.34.gains_ref, f32[4,392,512]{2,1,0:T(8,128)S(1)} %get-tuple-element.43.scale_ref, f32[4,384,512]{2,1,0:T(8,128)S(1)} %get-tuple-element.44.series_ref, ...), custom_call_target="tpu_custom_call" | custom-call | flops 2415919104 | bytes 16777216 | tf_op jit(solution)/shard_map/middle/pallas_call | solution.py:524
  33.9 1.8 %middle.5.refs_0_ = f32[16,384,128]{2,1,0:T(8,128)S(1)} custom-call(bf16[384,1024]{1,0:T(8,128)(2,1)S(1)} %collective-permute-done.2.section_ref, f32[8,2048]{1,0:T(8,128)S(1)} %get-tuple-element.34.gains_ref, f32[4,392,512]{2,1,0:T(8,128)S(1)} %get-tuple-element.43.scale_ref, ...), custom_call_target="tpu_custom_call", output_to_operand_aliasing={{}: (8, {})} | custom-call | flops 2415919104 | bytes 16777216 | tf_op jit(solution)/shard_map/middle/pallas_call | solution.py:524
  35.7 2.6 %collective-permute-done.1.section_ref = bf16[384,512]{1,0:T(8,128)(2,1)S(1)} collective-permute-done((bf16[384,512]{1,0:T(8,128)(2,1)S(1)}, bf16[384,512]{1,0:T(8,128)(2,1)S(1)}, u32[]{:S(2)}, u32[]{:S(2)}) %collective-permute-start.1) | collective-permute-done | bytes 393248 | tf_op jit(solution)/shard_map/ppermute | solution.py:480
  38.4 1.8 %middle.6.refs_0_ = f32[16,384,128]{2,1,0:T(8,128)S(1)} custom-call(bf16[384,512]{1,0:T(8,128)(2,1)S(1)} %collective-permute-done.1.section_ref, f32[8,2048]{1,0:T(8,128)S(1)} %get-tuple-element.34.gains_ref, f32[4,392,512]{2,1,0:T(8,128)S(1)} %get-tuple-element.43.scale_ref, ...), custom_call_target="tpu_custom_call", output_to_operand_aliasing={{}: (8, {})} | custom-call | flops 2415919104 | bytes 16777216 | tf_op jit(solution)/shard_map/middle/pallas_call | solution.py:524
  40.2 2.4 %collective-permute-done.section_ref = bf16[384,512]{1,0:T(8,128)(2,1)S(1)} collective-permute-done((bf16[384,512]{1,0:T(8,128)(2,1)S(1)}, bf16[384,512]{1,0:T(8,128)(2,1)S(1)}, u32[]{:S(2)}, u32[]{:S(2)}) %collective-permute-start) | collective-permute-done | bytes 393248 | tf_op jit(solution)/shard_map/ppermute | solution.py:480
  42.6 1.8 %middle.7.states_ref = f32[16,384,128]{2,1,0:T(8,128)S(1)} custom-call(bf16[384,512]{1,0:T(8,128)(2,1)S(1)} %collective-permute-done.section_ref, f32[8,2048]{1,0:T(8,128)S(1)} %get-tuple-element.34.gains_ref, f32[4,392,512]{2,1,0:T(8,128)S(1)} %get-tuple-element.43.scale_ref, ...), custom_call_target="tpu_custom_call", output_to_operand_aliasing={{}: (8, {})} | custom-call | flops 2415919104 | bytes 16777216 | tf_op jit(solution)/shard_map/middle/pallas_call | solution.py:524
  44.4 1.9 %last.1 = f32[384,2048]{1,0:T(8,128)} custom-call(f32[16,384,128]{2,1,0:T(8,128)S(1)} %middle.7.states_ref, f32[8,2048]{1,0:T(8,128)S(1)} %get-tuple-element.34.gains_ref, f32[384,128]{1,0:T(8,128)S(1)} %get-tuple-element.48.powers_ref, f32[4,2048]{1,0:T(4,128)S(1)} %get-tuple-element.59.sent_ref, f32[3,2048]{1,0:T(4,128)S(1)} %get-tuple-element.60.before_ref), custom_call_target="tpu_custom_call" | custom-call | flops 603979776 | bytes 16777216 | tf_op jit(solution)/shard_map/last/pallas_call | solution.py:555
  (4 shorter events, 0.2 us)
Async XLA Ops:
  0.0 3.4 %copy-start = (f32[384]{0:T(512)S(1)}, f32[384]{0:T(512)}, u32[]{:S(2)}) copy-start(f32[384]{0:T(512)} %burst_hbm.1) | copy-start | bytes 4612
  2.8 29.3 %collective-permute-start.2 = (bf16[384,1024]{1,0:T(8,128)(2,1)S(1)}, bf16[384,1024]{1,0:T(8,128)(2,1)S(1)}, u32[]{:S(2)}, u32[]{:S(2)}) collective-permute-start(bf16[384,1024]{1,0:T(8,128)(2,1)S(1)} %get-tuple-element.35.part_ref), channel_id=1, source_target_pairs={{0,2},{2,4},{4,6},{6,8},{8,10},{10,12},{12,14},{14,16},{16,18},{18... | collective-permute-start | bytes 2359304 | tf_op jit(solution)/shard_map/ppermute | solution.py:480
  3.4 12.9 %collective-permute-start.3 = (f32[384]{0:T(512)S(1)}, f32[384]{0:T(512)S(1)}, u32[]{:S(2)}, u32[]{:S(2)}) collective-permute-start(f32[384]{0:T(512)S(1)} %copy-done), channel_id=1, source_target_pairs={{2,0},{4,2},{6,4},{8,6},{10,8},{12,10},{14,12},{16,14},{18,16},{20... | collective-permute-start | bytes 4616 | tf_op jit(solution)/shard_map/ppermute | solution.py:481
  17.8 1.3 %collective-permute-start.4 = (f32[4,2048]{1,0:T(4,128)S(1)}, f32[4,2048]{1,0:T(4,128)S(1)}, u32[]{:S(2)}, u32[]{:S(2)}) collective-permute-start(f32[4,2048]{1,0:T(4,128)S(1)} %next.1.sent_ref), channel_id=1, source_target_pairs={{0,2},{2,0},{4,6},{6,4},{8,10},{10,8},{12,14},{14,12},{16,18},{18,... | collective-permute-start | bytes 98312 | tf_op jit(solution)/shard_map/ppermute | solution.py:542
  19.1 4.0 %collective-permute-start.5 = (f32[4,2048]{1,0:T(4,128)S(1)}, f32[4,2048]{1,0:T(4,128)S(1)}, u32[]{:S(2)}, u32[]{:S(2)}) collective-permute-start(f32[4,2048]{1,0:T(4,128)S(1)} %get-tuple-element.53.sent_ref), channel_id=1, source_target_pairs={{0,4},{2,6},{4,0},{6,2},{8,12},{10,14},{12,8},{14,10},{16,20},{18,... | collective-permute-start | bytes 98312 | tf_op jit(solution)/shard_map/ppermute | solution.py:542
  23.2 4.0 %collective-permute-start.6 = (f32[4,2048]{1,0:T(4,128)S(1)}, f32[4,2048]{1,0:T(4,128)S(1)}, u32[]{:S(2)}, u32[]{:S(2)}) collective-permute-start(f32[4,2048]{1,0:T(4,128)S(1)} %get-tuple-element.55.sent_ref), channel_id=1, source_target_pairs={{0,8},{2,10},{4,12},{6,14},{8,0},{10,2},{12,4},{14,6},{16,24},{18,... | collective-permute-start | bytes 98312 | tf_op jit(solution)/shard_map/ppermute | solution.py:542
  27.2 4.9 %collective-permute-start.7 = (f32[4,2048]{1,0:T(4,128)S(1)}, f32[4,2048]{1,0:T(4,128)S(1)}, u32[]{:S(2)}, u32[]{:S(2)}) collective-permute-start(f32[4,2048]{1,0:T(4,128)S(1)} %get-tuple-element.57.sent_ref), channel_id=1, source_target_pairs={{0,16},{2,18},{4,20},{6,22},{8,24},{10,26},{12,28},{14,30},{16,0},... | collective-permute-start | bytes 98312 | tf_op jit(solution)/shard_map/ppermute | solution.py:542
  28.5 9.9 %collective-permute-start.1 = (bf16[384,512]{1,0:T(8,128)(2,1)S(1)}, bf16[384,512]{1,0:T(8,128)(2,1)S(1)}, u32[]{:S(2)}, u32[]{:S(2)}) collective-permute-start(bf16[384,512]{1,0:T(8,128)(2,1)S(1)} %get-tuple-element.47), channel_id=1, source_target_pairs={{0,2},{2,4},{4,6},{6,8},{8,10},{10,12},{12,14},{14,16},{16,18},{18... | collective-permute-start | bytes 1179656 | tf_op jit(solution)/shard_map/ppermute | solution.py:480
  28.5 14.1 %collective-permute-start = (bf16[384,512]{1,0:T(8,128)(2,1)S(1)}, bf16[384,512]{1,0:T(8,128)(2,1)S(1)}, u32[]{:S(2)}, u32[]{:S(2)}) collective-permute-start(bf16[384,512]{1,0:T(8,128)(2,1)S(1)} %get-tuple-element.33), channel_id=1, source_target_pairs={{0,2},{2,4},{4,6},{6,8},{8,10},{10,12},{12,14},{14,16},{16,18},{18... | collective-permute-start | bytes 1179656 | tf_op jit(solution)/shard_map/ppermute | solution.py:480
